TPU v7x, 32 devices: a whole 2x2x4 slice. The times are simulated.
32 devices in a mesh: band: 4 (over y, core), grid: 8 (over z, x).
Axes of the slice: x: 2, y: 2, z: 4, core: 2. Of those that a mesh axis runs over, the one named last changes fastest.
Arguments:
- orbitals: bfloat16 [64, 2, 16, 128, 128], P('band', None, 'grid'), may hold values from -1.5 to 1.5
- occupations: float32 [64], P('band'), may hold values from 0.2 to 2
Outputs:
- current: float32 [3, 16, 128, 128], P(None, 'grid', 'band')
All inputs are finite; a program needn't handle non-finite values.
Results may differ from a plain program's by a relative error of at most 0.0003.
Values may be sent and summed in bfloat16 or wider, within the bound.
No kernel may reach another device: no remote copies, remote signals or barrier semaphores. Data moves between devices by JAX's collectives and lax.ppermute only.
A program may use at most 64 MiB of HBM per device.

v0:
```python
import math

import jax
import jax.numpy as jnp
from jax import lax
from jax.sharding import PartitionSpec as P


def extended(cells, sides, width):
    for axis, dim in sides:
        count = lax.axis_size(axis)
        head = lax.slice_in_dim(cells, 0, width, axis=dim)
        tail = lax.slice_in_dim(cells, cells.shape[dim] - width, cells.shape[dim], axis=dim)
        cells = jnp.concatenate(
            [
                lax.ppermute(tail, axis, [(i, (i + 1) % count) for i in range(count)]),
                cells,
                lax.ppermute(head, axis, [((i + 1) % count, i) for i in range(count)]),
            ],
            axis=dim,
        )
    return cells


def derivative(values, direction):
    forward = jnp.roll(values, -1, direction) - jnp.roll(values, 1, direction)
    farther = jnp.roll(values, -2, direction) - jnp.roll(values, 2, direction)
    return (8.0 * forward - farther) / 12.0


def vertical(widened, depth_cells):
    forward = widened[:, 3 : 3 + depth_cells] - widened[:, 1 : 1 + depth_cells]
    farther = widened[:, 4 : 4 + depth_cells] - widened[:, 0:depth_cells]
    return (8.0 * forward - farther) / 12.0


def band_sum(orbitals, weights, padded, with_depth, lateral):
    bands = orbitals.shape[0]
    depth_cells = orbitals.shape[2]
    block_size = math.gcd(bands, 8)
    parts_count = (1 if with_depth else 0) + (2 if lateral else 0)

    def advance(block_index, summed):
        offset = block_index * block_size
        center = lax.dynamic_slice_in_dim(orbitals, offset, block_size, 0).astype(jnp.float32)
        factors = lax.dynamic_slice_in_dim(weights, offset, block_size, 0)
        real_part = center[:, 0]
        imag_part = center[:, 1]
        terms = []
        if with_depth:
            widened = lax.dynamic_slice_in_dim(padded, offset, block_size, 0).astype(jnp.float32)
            terms.append(
                real_part * vertical(widened[:, 1], depth_cells)
                - imag_part * vertical(widened[:, 0], depth_cells)
            )
        if lateral:
            for direction in (2, 3):
                terms.append(
                    real_part * derivative(imag_part, direction)
                    - imag_part * derivative(real_part, direction)
                )
        stacked = jnp.stack(terms)
        return summed + jnp.sum(factors[None, :, None, None, None] * stacked, 1)

    initial = jnp.zeros(
        (parts_count, depth_cells, orbitals.shape[3], orbitals.shape[4]), jnp.float32
    )
    return lax.fori_loop(0, bands // block_size, advance, initial)


def depth_part(orbitals, weights):
    padded = extended(orbitals, (("grid", 2),), 2)
    return band_sum(orbitals, weights, padded, True, False)


def per_device(orbitals, occupations):
    lateral_part = band_sum(orbitals, occupations, None, False, True)
    plane_sums = lax.psum_scatter(lateral_part, "band", scatter_dimension=2, tiled=True)
    depth_sums = lax.psum_scatter(
        depth_part(orbitals, occupations), "band", scatter_dimension=2, tiled=True
    )
    return jnp.concatenate([depth_sums, plane_sums], 0)


def solution(mesh):
    placed = (P("band", None, "grid", None, None), P("band"))
    return jax.shard_map(
        per_device,
        mesh=mesh,
        in_specs=placed,
        out_specs=P(None, "grid", "band", None),
        check_vma=False,
    )
```

profile of v0, /device:TPU:0, one launch (start us, length us, event | category | flops | bytes accessed | tf_op | source)
XLA Modules:
  0.0 149.4 jit_solution(17086221204871014268)
XLA Ops:
  6.5 3.3 %copy.34 = bf16[16,2,2,128,128]{4,3,2,0,1:T(8,128)(2,1)} copy(bf16[16,2,2,128,128]{4,3,2,1,0:T(8,128)(2,1)} %param.6) | data formatting | bytes 4194304 | tf_op args[0]
  9.9 6.0 %collective-permute-start.1 = (bf16[16,2,2,128,128]{4,3,2,0,1:T(8,128)(2,1)}, bf16[16,2,2,128,128]{4,3,2,0,1:T(8,128)(2,1)}, u32[]{:S(2)}, u32[]{:S(2)}) collective-permute-start(bf16[16,2,2,128,128]{4,3,2,0,1:T(8,128)(2,1)} %copy.34), channel_id=1, source_target_pairs={{1,0},{2,1},{3,2},{4,3},{5,4},{6,5},{7,6},{0,7},{9,8},{10,9},{11,1... | collective-permute-start | bytes 6291464 | tf_op jit(solution)/shard_map/ppermute | solution.py:18
  15.9 66.2 %while.29 = (s32[]{:T(128)}, f32[2,2,128,128]{3,2,1,0:T(8,128)S(1)}, f32[16]{0:T(128)S(1)}, bf16[16,2,2,128,128]{4,3,2,1,0:T(8,128)(2,1)S(1)}, s32[]{:T(128)}, /...) while((s32[]{:T(128)}, f32[2,2,128,128]{3,2,1,0:T(8,128)S(1)}, ...), condition=%wide.region_6.7_spmd.clone, body=%wide.region_4.6_spmd.clone.sunk | while | flops 13172743 | bytes 94503256 | solution.py:68
  15.9 0.1 constant_dynamic-slice_fusion.2
  16.0 0.6 copy_convert_fusion.2
  16.6 0.1 slice_bitcast_fusion.44
  16.8 1.2 copy-done
  18.0 2.3 %fusion.42 = (f32[8,2,128,1]{3,0,2,1:T(8,128)}, f32[8,2,128,1]{3,0,2,1:T(8,128)}, f32[8,2,128,1]{3,0,2,1:T(8,128)S(1)}, f32[8,2,128,1]{3,0,2,1:T(8,128)}) fusion(f32[8,2,128,128]{3,0,2,1:T(8,128)S(1)} %get-tuple-element.385, f32[8,2,128,128]{3,0,2,1:T(8,128)S(1)} %get-tuple-element.386), kind=kLoop, calls=%fused_computation.85.clone.1 | loop fusion | bytes 65536 | tf_op jit(solution)/shard_map/while/body/eval_jaxpr/jit(_roll_static)/slice | solution.py:26
  20.2 0.4 copy.56
  20.6 0.4 copy.57
  21.0 2.5 %slice_bitcast_fusion.45 = (f32[1,8,2,128,127]{4,1,3,2,0:T(8,128)}, f32[1,8,2,128,127]{4,1,3,2,0:T(8,128)}, f32[1,8,2,128,127]{4,1,3,2,0:T(8,128)}, f32[1,8,2,128,127]{4,1,3,2,0:T(8,128)}) fusion(f32[8,2,128,128]{3,0,2,1:T(8,128)S(1)} %get-tuple-element.385, f32[8,2,128,128]{3,0,2,1:T(8,128)S(1)} %get-tuple-element.386), kind=kLoop, calls=%fused_computation.28.clone.1 | loop fusion | bytes 8323072 | tf_op jit(solution)/shard_map/while/body/eval_jaxpr/jit(_roll_static)/concatenate | solution.py:26
  23.6 1.6 %copy.58 = f32[8,2,128,1]{2,0,3,1:T(8,128)S(1)} copy(f32[8,2,128,1]{3,0,2,1:T(8,128)} %get-tuple-element.390) | data formatting | bytes 16384 | tf_op jit(solution)/shard_map/while/body/eval_jaxpr/jit(_roll_static)/slice | solution.py:26
  25.1 1.4 copy.59
  26.5 2.6 %slice_bitcast_fusion.46 = (f32[1,8,2,128,2]{4,1,3,2,0:T(8,128)}, f32[1,8,2,128,2]{4,1,3,2,0:T(8,128)}, f32[1,8,2,128,2]{4,1,3,2,0:T(8,128)}, f32[1,8,2,128,2]{4,1,3,2,0:T(8,128)}) fusion(f32[8,2,128,128]{3,0,2,1:T(8,128)S(1)} %get-tuple-element.385, f32[8,2,128,128]{3,0,2,1:T(8,128)S(1)} %get-tuple-element.386), kind=kLoop, calls=%fused_computation.25.clone.1 | loop fusion | bytes 131072 | tf_op jit(solution)/shard_map/while/body/eval_jaxpr/jit(_roll_static)/concatenate | solution.py:27
  29.0 2.6 %slice_bitcast_fusion.47 = (f32[1,8,2,128,126]{4,1,3,2,0:T(8,128)}, f32[1,8,2,128,126]{4,1,3,2,0:T(8,128)}, f32[1,8,2,128,126]{4,1,3,2,0:T(8,128)}, f32[1,8,2,128,126]{4,1,3,2,0:T(8,128)}) fusion(f32[8,2,128,128]{3,0,2,1:T(8,128)S(1)} %get-tuple-element.385, f32[8,2,128,128]{3,0,2,1:T(8,128)S(1)} %get-tuple-element.386), kind=kLoop, calls=%fused_computation.24.clone.1 | loop fusion | bytes 8257536 | tf_op jit(solution)/shard_map/while/body/eval_jaxpr/jit(_roll_static)/concatenate | solution.py:27
  31.7 1.6 %copy.60 = f32[8,2,128,1]{2,0,3,1:T(8,128)S(1)} copy(f32[8,2,128,1]{3,0,2,1:T(8,128)} %get-tuple-element.395) | data formatting | bytes 16384 | tf_op jit(solution)/shard_map/while/body/eval_jaxpr/jit(_roll_static)/slice | solution.py:26
  33.2 1.4 copy.61
  34.6 1.6 %copy.62 = f32[8,2,128,1]{2,0,3,1:T(8,128)S(1)} copy(f32[8,2,128,1]{3,0,2,1:T(8,128)} %get-tuple-element.398) | data formatting | bytes 16384 | tf_op jit(solution)/shard_map/while/body/eval_jaxpr/jit(_roll_static)/slice | solution.py:26
  36.2 1.4 copy.63
  37.6 7.3 %fusion.43 = f32[1,8,2,128,128]{4,1,3,2,0:T(8,128)S(1)} fusion(f32[1,8,2,128,1]{4,1,3,2,0:T(8,128)S(1)} %copy.57, f32[1,8,2,128,127]{4,1,3,2,0:T(8,128)} %get-tuple-element.388, f32[1,8,2,128,127]{4,1,3,2,0:T(8,128)} %get-tuple-element.389, f32[1,8,2,128,1]{4,1,3,2,0:T(8,128)} %copy.59, f32[1,8,2,128,2]{4,1,3,2,0:T(8,128)} %get-tuple-element.391, ...), kind=kLoop, calls=%fused_computation.54.clone.1 | loop fusion | flops 5505024 | bytes 11534336 | tf_op jit(solution)/shard_map/while/body/eval_jaxpr/sub | solution.py:59
  44.9 0.3 slice_bitcast_fusion.49
  45.2 0.3 slice_bitcast_fusion.51
  45.5 1.3 copy-done.1
  46.8 0.6 fusion.44
  47.5 0.7 fusion.45
  48.3 0.7 copy-done.3
  49.1 0.6 copy_convert_fusion.2
  49.7 0.1 slice_bitcast_fusion.44
  49.9 1.2 copy-done
  51.0 2.3 %fusion.42 = (f32[8,2,128,1]{3,0,2,1:T(8,128)}, f32[8,2,128,1]{3,0,2,1:T(8,128)}, f32[8,2,128,1]{3,0,2,1:T(8,128)S(1)}, f32[8,2,128,1]{3,0,2,1:T(8,128)}) fusion(f32[8,2,128,128]{3,0,2,1:T(8,128)S(1)} %get-tuple-element.385, f32[8,2,128,128]{3,0,2,1:T(8,128)S(1)} %get-tuple-element.386), kind=kLoop, calls=%fused_computation.85.clone.1 | loop fusion | bytes 65536 | tf_op jit(solution)/shard_map/while/body/eval_jaxpr/jit(_roll_static)/slice | solution.py:26
  53.3 0.4 copy.56
  53.7 0.4 copy.57
  54.1 2.5 %slice_bitcast_fusion.45 = (f32[1,8,2,128,127]{4,1,3,2,0:T(8,128)}, f32[1,8,2,128,127]{4,1,3,2,0:T(8,128)}, f32[1,8,2,128,127]{4,1,3,2,0:T(8,128)}, f32[1,8,2,128,127]{4,1,3,2,0:T(8,128)}) fusion(f32[8,2,128,128]{3,0,2,1:T(8,128)S(1)} %get-tuple-element.385, f32[8,2,128,128]{3,0,2,1:T(8,128)S(1)} %get-tuple-element.386), kind=kLoop, calls=%fused_computation.28.clone.1 | loop fusion | bytes 8323072 | tf_op jit(solution)/shard_map/while/body/eval_jaxpr/jit(_roll_static)/concatenate | solution.py:26
  56.7 1.6 %copy.58 = f32[8,2,128,1]{2,0,3,1:T(8,128)S(1)} copy(f32[8,2,128,1]{3,0,2,1:T(8,128)} %get-tuple-element.390) | data formatting | bytes 16384 | tf_op jit(solution)/shard_map/while/body/eval_jaxpr/jit(_roll_static)/slice | solution.py:26
  58.2 1.4 copy.59
  59.6 2.6 %slice_bitcast_fusion.46 = (f32[1,8,2,128,2]{4,1,3,2,0:T(8,128)}, f32[1,8,2,128,2]{4,1,3,2,0:T(8,128)}, f32[1,8,2,128,2]{4,1,3,2,0:T(8,128)}, f32[1,8,2,128,2]{4,1,3,2,0:T(8,128)}) fusion(f32[8,2,128,128]{3,0,2,1:T(8,128)S(1)} %get-tuple-element.385, f32[8,2,128,128]{3,0,2,1:T(8,128)S(1)} %get-tuple-element.386), kind=kLoop, calls=%fused_computation.25.clone.1 | loop fusion | bytes 131072 | tf_op jit(solution)/shard_map/while/body/eval_jaxpr/jit(_roll_static)/concatenate | solution.py:27
  62.1 2.6 %slice_bitcast_fusion.47 = (f32[1,8,2,128,126]{4,1,3,2,0:T(8,128)}, f32[1,8,2,128,126]{4,1,3,2,0:T(8,128)}, f32[1,8,2,128,126]{4,1,3,2,0:T(8,128)}, f32[1,8,2,128,126]{4,1,3,2,0:T(8,128)}) fusion(f32[8,2,128,128]{3,0,2,1:T(8,128)S(1)} %get-tuple-element.385, f32[8,2,128,128]{3,0,2,1:T(8,128)S(1)} %get-tuple-element.386), kind=kLoop, calls=%fused_computation.24.clone.1 | loop fusion | bytes 8257536 | tf_op jit(solution)/shard_map/while/body/eval_jaxpr/jit(_roll_static)/concatenate | solution.py:27
  64.8 1.6 %copy.60 = f32[8,2,128,1]{2,0,3,1:T(8,128)S(1)} copy(f32[8,2,128,1]{3,0,2,1:T(8,128)} %get-tuple-element.395) | data formatting | bytes 16384 | tf_op jit(solution)/shard_map/while/body/eval_jaxpr/jit(_roll_static)/slice | solution.py:26
  66.3 1.4 copy.61
  67.7 1.6 %copy.62 = f32[8,2,128,1]{2,0,3,1:T(8,128)S(1)} copy(f32[8,2,128,1]{3,0,2,1:T(8,128)} %get-tuple-element.398) | data formatting | bytes 16384 | tf_op jit(solution)/shard_map/while/body/eval_jaxpr/jit(_roll_static)/slice | solution.py:26
  69.3 1.4 copy.63
  70.7 7.3 %fusion.43 = f32[1,8,2,128,128]{4,1,3,2,0:T(8,128)S(1)} fusion(f32[1,8,2,128,1]{4,1,3,2,0:T(8,128)S(1)} %copy.57, f32[1,8,2,128,127]{4,1,3,2,0:T(8,128)} %get-tuple-element.388, f32[1,8,2,128,127]{4,1,3,2,0:T(8,128)} %get-tuple-element.389, f32[1,8,2,128,1]{4,1,3,2,0:T(8,128)} %copy.59, f32[1,8,2,128,2]{4,1,3,2,0:T(8,128)} %get-tuple-element.391, ...), kind=kLoop, calls=%fused_computation.54.clone.1 | loop fusion | flops 5505024 | bytes 11534336 | tf_op jit(solution)/shard_map/while/body/eval_jaxpr/sub | solution.py:59
  78.0 0.3 slice_bitcast_fusion.49
  78.3 0.3 slice_bitcast_fusion.51
  78.6 1.3 copy-done.1
  79.9 0.6 fusion.44
  80.6 0.7 fusion.45
  81.4 0.7 copy-done.3
  82.1 0.7 copy-done.4
  82.9 20.8 %collective-permute-done.1 = bf16[16,2,2,128,128]{4,3,2,0,1:T(8,128)(2,1)} collective-permute-done((bf16[16,2,2,128,128]{4,3,2,0,1:T(8,128)(2,1)}, bf16[16,2,2,128,128]{4,3,2,0,1:T(8,128)(2,1)}, u32[]{:S(2)}, u32[]{:S(2)}) %collective-permute-start.1) | collective-permute-done | bytes 2097184 | tf_op jit(solution)/shard_map/ppermute | solution.py:18
  103.7 0.2 collective-permute-done
  103.9 5.4 %pad_maximum_fusion = bf16[16,2,6,128,128]{4,3,2,0,1:T(8,128)(2,1)} fusion(bf16[16,2,2,128,128]{4,3,2,0,1:T(8,128)(2,1)} %collective-permute-done.1, bf16[16,2,2,128,128]{4,3,2,0,1:T(8,128)(2,1)} %collective-permute-done, bf16[16,2,2,128,128]{4,3,2,1,0:T(8,128)(2,1)S(1)} %get-tuple-element.475), kind=kLoop, calls=%fused_computation.83 | loop fusion | flops 18874368 | bytes 12582912 | tf_op jit(solution)/shard_map/concatenate | solution.py:14
  109.3 9.7 %while.28 = (s32[]{:T(128)}, f32[1,2,128,128]{3,2,1,0:T(8,128)S(1)}, f32[16]{0:T(128)S(1)}, bf16[16,2,2,128,128]{4,3,2,1,0:T(8,128)(2,1)S(1)}, bf16[16,2,6,128,1...) while((s32[]{:T(128)}, f32[1,2,128,128]{3,2,1,0:T(8,128)S(1)}, ...), condition=%wide.region_2.3_spmd.clone, body=%wide.region_0.2_spmd.clone.sunk | while | flops 6062087 | bytes 36176136 | solution.py:68
  109.3 2.7 %dynamic-slice_convert_fusion.4 = f32[8,2,6,128,128]{4,3,2,0,1:T(8,128)S(1)} fusion(bf16[16,2,6,128,128]{4,3,2,0,1:T(8,128)(2,1)} %get-tuple-element.465, s32[]{:T(128)S(6)} %select_n.21), kind=kLoop, calls=%fused_computation.2.clone.1 | loop fusion | flops 1572864 | bytes 9437188 | tf_op jit(solution)/shard_map/while/body/eval_jaxpr/convert_element_type | solution.py:51
  112.0 0.8 slice_bitcast_fusion.43
  112.8 0.2 dynamic-slice_convert_fusion.5
  113.1 1.0 fusion.41
  114.2 2.7 %dynamic-slice_convert_fusion.4 = f32[8,2,6,128,128]{4,3,2,0,1:T(8,128)S(1)} fusion(bf16[16,2,6,128,128]{4,3,2,0,1:T(8,128)(2,1)} %get-tuple-element.465, s32[]{:T(128)S(6)} %select_n.21), kind=kLoop, calls=%fused_computation.2.clone.1 | loop fusion | flops 1572864 | bytes 9437188 | tf_op jit(solution)/shard_map/while/body/eval_jaxpr/convert_element_type | solution.py:51
  116.9 0.8 slice_bitcast_fusion.43
  117.7 0.2 dynamic-slice_convert_fusion.5
  118.0 1.0 fusion.41
  119.0 0.6 copy-done.5
  119.7 21.4 %reduce-scatter.3.cloned.1.call-done = f32[1,2,32,128]{3,2,1,0:T(8,128)} async-done(((f32[1,2,128,128]{3,2,1,0:T(8,128)}), f32[1,2,32,128]{3,2,1,0:T(8,128)}) %reduce-scatter.3.cloned.1.call-update) | async-done | bytes 32784 | tf_op jit(solution)/shard_map/reduce_scatter | solution.py:79
  141.1 1.5 pad_maximum_fusion.1
  (33 shorter events, 0.8 us)
Async XLA Ops:
  6.5 9.3 %copy-start.2 = (bf16[16,2,2,128,128]{4,3,2,1,0:T(8,128)(2,1)S(1)}, bf16[16,2,2,128,128]{4,3,2,1,0:T(8,128)(2,1)}, u32[]{:S(2)}) copy-start(bf16[16,2,2,128,128]{4,3,2,1,0:T(8,128)(2,1)} %param.6) | copy-start | bytes 6291460
  6.5 9.3 %copy-start.6 = (f32[16]{0:T(128)S(1)}, f32[16]{0:T(128)}, u32[]{:S(2)}) copy-start(f32[16]{0:T(128)} %param.7) | copy-start | bytes 196
  6.5 113.2 %reduce-scatter.5.cloned.1.call-start = ((), (), s32[]{:S(2)}) async-start(), calls=%async_computation.3 | async-start | bytes 327680 | tf_op jit(solution)/shard_map/reduce_scatter | solution.py:78
  9.9 93.9 %collective-permute-start.1 = (bf16[16,2,2,128,128]{4,3,2,0,1:T(8,128)(2,1)}, bf16[16,2,2,128,128]{4,3,2,0,1:T(8,128)(2,1)}, u32[]{:S(2)}, u32[]{:S(2)}) collective-permute-start(bf16[16,2,2,128,128]{4,3,2,0,1:T(8,128)(2,1)} %copy.34), channel_id=1, source_target_pairs={{1,0},{2,1},{3,2},{4,3},{5,4},{6,5},{7,6},{0,7},{9,8},{10,9},{11,1... | collective-permute-start | bytes 6291464 | tf_op jit(solution)/shard_map/ppermute | solution.py:18
  15.9 88.0 %collective-permute-start = (bf16[16,2,2,128,128]{4,3,2,0,1:T(8,128)(2,1)}, bf16[16,2,2,128,128]{4,3,2,0,1:T(8,128)(2,1)}, u32[]{:S(2)}, u32[]{:S(2)}) collective-permute-start(bf16[16,2,2,128,128]{4,3,2,0,1:T(8,128)(2,1)} %copy.34), channel_id=1, source_target_pairs={{0,1},{1,2},{2,3},{3,4},{4,5},{5,6},{6,7},{7,0},{8,9},{9,10},{10,1... | collective-permute-start | bytes 6291464 | tf_op jit(solution)/shard_map/ppermute | solution.py:16
  16.6 1.3 copy-start
  45.2 1.6 %copy-start.1 = (f32[8,2,2,128,128]{4,0,3,2,1:T(8,128)S(1)}, f32[8,2,2,128,128]{4,0,3,2,1:T(8,128)}, u32[]{:S(2)}) copy-start(f32[8,2,2,128,128]{4,0,3,2,1:T(8,128)} %copy-done) | copy-start | bytes 6291460 | tf_op jit(solution)/shard_map/while
  47.4 1.6 %copy-start.3 = (bf16[16,2,2,128,128]{4,3,2,1,0:T(8,128)(2,1)S(1)}, bf16[16,2,2,128,128]{4,3,2,1,0:T(8,128)(2,1)}, u32[]{:S(2)}) copy-start(bf16[16,2,2,128,128]{4,3,2,1,0:T(8,128)(2,1)} %get-tuple-element.480) | copy-start | bytes 6291460 | tf_op jit(solution)/shard_map/while
  49.7 1.3 copy-start
  78.3 1.6 %copy-start.1 = (f32[8,2,2,128,128]{4,0,3,2,1:T(8,128)S(1)}, f32[8,2,2,128,128]{4,0,3,2,1:T(8,128)}, u32[]{:S(2)}) copy-start(f32[8,2,2,128,128]{4,0,3,2,1:T(8,128)} %copy-done) | copy-start | bytes 6291460 | tf_op jit(solution)/shard_map/while
  80.5 1.6 %copy-start.3 = (bf16[16,2,2,128,128]{4,3,2,1,0:T(8,128)(2,1)S(1)}, bf16[16,2,2,128,128]{4,3,2,1,0:T(8,128)(2,1)}, u32[]{:S(2)}) copy-start(bf16[16,2,2,128,128]{4,3,2,1,0:T(8,128)(2,1)} %get-tuple-element.480) | copy-start | bytes 6291460 | tf_op jit(solution)/shard_map/while
  82.1 0.7 copy-start.4
  82.8 58.3 %reduce-scatter.3.cloned.1.call-start = ((), (), s32[]{:S(2)}) async-start(), calls=%async_computation.2 | async-start | bytes 163840 | tf_op jit(solution)/shard_map/reduce_scatter | solution.py:79
  119.0 0.7 copy-start.5
Sparse Core Ops, SparseCore 0:
  83.0 21.4 reduce-scatter.4
  119.8 21.2 reduce-scatter.2
where the time goes:
time: 150 us; the launch traced here: 149 us
  local copies, waits for them, and re-layouts  53.9 us (36%)
  waiting for transfers between devices  42.4 us (28%)
  other arithmetic  33.3 us (22%)
  between operations  13.4 us (9%)
  starting transfers between devices  6.05 us (4%)
    reduce_scatter x1, waiting for transfers between devices, per_device(): lax.psum_scatter(depth_part(orbitals, occupations), 'band', scatter_dimen...  21.4 us
    ppermute x1, waiting for transfers between devices, extended(): lax.ppermute(head, axis, [((i + 1) % count, i) for i in range(count)])  20.8 us
    sub x4, other arithmetic, advance(): real_part * derivative(imag_part, direction)  15.8 us
    concatenate x14, local copies, waits for them, and re-layouts, derivative(): forward = jnp.roll(values, -1, direction) - jnp.roll(values, 1, direction)  14.9 us
    slice x10, local copies, waits for them, and re-layouts, derivative(): forward = jnp.roll(values, -1, direction) - jnp.roll(values, 1, direction)  14.6 us
    concatenate x8, local copies, waits for them, and re-layouts, derivative(): farther = jnp.roll(values, -2, direction) - jnp.roll(values, 2, direction)  10.9 us
    while x12, local copies, waits for them, and re-layouts  6.42 us
    ppermute x1, starting transfers between devices, extended(): lax.ppermute(head, axis, [((i + 1) % count, i) for i in range(count)])  6 us
  transfers between devices with their start and end apart: 4, of which 3 were waited for; matrix products, arithmetic and copies ran while one was open for 50% of the time, Pallas kernels for 0%

commit v1 on v0

v1 whole, which is shorter than its diff:
```python
import functools

import jax
import jax.numpy as jnp
import numpy as np
from jax import lax
from jax.experimental import pallas as pl
from jax.experimental.pallas import tpu as pltpu
from jax.sharding import PartitionSpec as P


def stencil(cells):
    eye = np.eye(cells, dtype=np.float32)
    near = np.roll(eye, 1, 0) - np.roll(eye, -1, 0)
    far = np.roll(eye, 2, 0) - np.roll(eye, -2, 0)
    return jnp.asarray(8.0 * near - far, jnp.bfloat16)


def lateral_kernel(weights, block, across, along, out, total):
    step = pl.program_id(0)

    @pl.when(step == 0)
    def _():
        total[...] = jnp.zeros_like(total)

    weight = weights[step]
    fields = []
    for plane in range(2):
        re16 = block[0, 0, plane]
        im16 = block[0, 1, plane]
        re = weight * re16.astype(jnp.float32)
        im = weight * im16.astype(jnp.float32)
        fields.append((re, im, re16, im16))
        dot = functools.partial(jnp.dot, preferred_element_type=jnp.float32)
        total[1 + plane] += re * dot(across[...], im16) - im * dot(across[...], re16)
        total[3 + plane] += re * dot(im16, along[...]) - im * dot(re16, along[...])
    (re, im, _, _), (_, _, re_up, im_up) = fields
    total[0] += 8.0 * (re * im_up.astype(jnp.float32) - im * re_up.astype(jnp.float32))

    @pl.when(step == pl.num_programs(0) - 1)
    def _():
        rows = out.shape[3]
        for core in range(2):
            for half in range(2):
                at = (2 * half + core) * rows
                out[core, half] = total[:, at : at + rows] * (1.0 / 12.0)


def lateral(orbitals, weights):
    bands, parts, planes, nx, ny = orbitals.shape
    return pl.pallas_call(
        lateral_kernel,
        grid=(bands,),
        in_specs=[
            pl.BlockSpec(memory_space=pltpu.SMEM),
            pl.BlockSpec((1, parts, planes, nx, ny), lambda n: (n, 0, 0, 0, 0)),
            pl.BlockSpec((nx, nx), lambda n: (0, 0)),
            pl.BlockSpec((ny, ny), lambda n: (0, 0)),
        ],
        out_specs=pl.BlockSpec((2, 2, 5, nx // 4, ny), lambda n: (0, 0, 0, 0, 0)),
        out_shape=jax.ShapeDtypeStruct((2, 2, 5, nx // 4, ny), jnp.float32),
        scratch_shapes=[pltpu.VMEM((5, nx, ny), jnp.float32)],
        name="lateral",
    )(weights, orbitals, stencil(nx).T, stencil(ny))


def crossing(weight_sets, first_sets, second_sets, odd):
    rows, lanes = first_sets[0].shape[-2:]
    zero = jnp.zeros((rows, lanes), jnp.float32)
    sums = (zero, zero, zero)
    for weights, first, second in zip(weight_sets, first_sets, second_sets):

        def advance(n, sums):
            def pair(lower, upper):
                re, im = (weights[n] * first[n, part, lower].astype(jnp.float32) for part in range(2))
                re_up, im_up = (second[n, part, upper].astype(jnp.float32) for part in range(2))
                return re * im_up - im * re_up

            return (
                sums[0] + pair(0, 0),
                sums[1] + pair(1, 1),
                sums[2] + pair(1 - odd, odd),
            )

        sums = lax.fori_loop(0, first.shape[0], advance, sums, unroll=2)
    sign = (1 - 2 * odd).astype(jnp.float32) * (1.0 / 12.0)
    return sign * sums[0], sign * sums[1], (8.0 * sign) * sums[2]


def inner_kernel(flags, w1, w2, own1, own2, side1, side2, own_out, side_out):
    odd = flags[0]
    low, high, mid = crossing((w1, w2), (own1, own2), (side1, side2), odd)
    up = jnp.where(odd == 1, 1.0, 0.0)
    own_out[0] = up * mid - low
    own_out[1] = (1.0 - up) * mid - high
    side_out[0] = (1.0 - up) * mid - low
    side_out[1] = up * mid - high


def outer_kernel(flags, w1, w2, side1, side2, far1, far2, own_in, side_in, kept, near, middle, distant):
    odd = flags[0]
    corner = flags[1]
    low, high, mid = crossing((w1, w2), (side1, side2), (far1, far2), odd)
    up = jnp.where(odd == 1, 1.0, 0.0)
    own = own_in[...]
    side = side_in[...] + jnp.stack([up * mid - low, (1.0 - up) * mid - high])
    far = jnp.stack([(1.0 - up) * mid - low, up * mid - high])
    here = corner == 1
    kept[...] = jnp.where(here, own, 0.0)
    near[...] = jnp.where(here, side, own)
    middle[...] = jnp.where(here, far, side)
    distant[...] = far


def call(kernel, scalars, arrays, outs):
    smem = pl.BlockSpec(memory_space=pltpu.SMEM)
    vmem = pl.BlockSpec(memory_space=pltpu.VMEM)
    shape = arrays[0].shape
    out = jax.ShapeDtypeStruct((2,) + shape[-2:], jnp.float32)
    return pl.pallas_call(
        kernel,
        in_specs=[smem] * len(scalars) + [vmem] * len(arrays),
        out_specs=[vmem] * outs,
        out_shape=[out] * outs,
        name=kernel.__name__,
    )(*scalars, *arrays)


def per_device(orbitals, occupations):
    slabs = lax.axis_size("grid")
    groups = lax.axis_size("band")
    assert groups == 4 and slabs % 2 == 0 and orbitals.shape[2] == 2
    slab = lax.axis_index("grid")
    group = lax.axis_index("band")
    odd = slab % 2
    core = group % 2
    half = group // 2
    corner = (half == odd).astype(jnp.int32)
    flags = jnp.stack([odd, corner]).astype(jnp.int32)
    quarter = orbitals.shape[3] // 4

    def beyond(g):
        return (g + 2) % slabs if g % 2 else (g - 2) % slabs

    def home(g):
        return (g - 2) % slabs if g % 2 else (g + 2) % slabs

    def route(value, target):
        pairs = []
        for b in range(groups):
            for g in range(slabs):
                goal = target(b, g)
                if goal is not None:
                    pairs.append((b * slabs + g, goal[0] * slabs + goal[1]))
        return lax.ppermute(value, ("band", "grid"), pairs)

    def rows(index):
        return lax.dynamic_slice_in_dim(orbitals, index * quarter, quarter, 3)

    own = rows(2 * odd + core)
    own_across = rows(2 * odd + 1 - core)
    side = rows(2 * (1 - odd) + core)
    side_across = rows(2 * (1 - odd) + 1 - core)

    w2 = route(occupations, lambda b, g: (b ^ 1, g))
    far1 = route(own, lambda b, g: (b, beyond(g)))
    side1 = route(side, lambda b, g: (b, g ^ 1))
    far2 = route(own_across, lambda b, g: (b ^ 1, beyond(g)))
    side2 = route(side_across, lambda b, g: (b ^ 1, g ^ 1))
    own2 = route(own_across, lambda b, g: (b ^ 1, g))

    flat = lateral(orbitals, occupations)
    flat = flat[core] + route(flat[1 - core], lambda b, g: (b ^ 1, g))
    flat = flat[half] + route(flat[1 - half], lambda b, g: (b ^ 2, g))

    weights = (occupations, w2)
    own_part, side_part = call(inner_kernel, (flags, *weights), (own, own2, side1, side2), 2)
    kept, near, middle, distant = call(
        outer_kernel,
        (flags, *weights),
        (side1, side2, far1, far2, own_part, side_part),
        4,
    )

    def is_corner(b, g):
        return b // 2 == g % 2

    got = route(distant, lambda b, g: None if is_corner(b, g) else (b ^ 2, home(g)))
    got_middle = route(
        middle, lambda b, g: (b, home(g)) if is_corner(b, g) else (b ^ 2, g ^ 1)
    )
    got_near = route(near, lambda b, g: (b, g ^ 1) if is_corner(b, g) else (b ^ 2, g))
    depth = flat[0][None] + kept + got_near + got_middle + got
    return jnp.stack([depth, flat[1:3], flat[3:5]])


def solution(mesh):
    placed = (P("band", None, "grid", None, None), P("band"))
    return jax.shard_map(
        per_device,
        mesh=mesh,
        in_specs=placed,
        out_specs=P(None, "grid", "band", None),
        check_vma=False,
    )
```

time: 150 us -> 66.2 us (0.44)
  local copies, waits for them, and re-layouts: 53.9 us -> 4.86 us
  other arithmetic: 33.3 us -> 2.95 us
  Pallas kernels: 0 us -> 16 us
  waiting for transfers between devices: 42.4 us -> 28.2 us
  between operations: 13.4 us -> 0.1 us
  starting transfers between devices: 6.05 us -> 13.6 us
    concatenate x22 -> x0, local copies, waits for them, and re-layouts: 25.8 us -> none  [the longest x14 14.9 us: derivative(): forward = jnp.roll(values, -1, direction) - jnp.roll(values, 1, direction)]
    reduce_scatter x2 -> x0, waiting for transfers between devices: 21.4 us -> none  [the longest x1 21.4 us: per_device(): lax.psum_scatter(depth_part(orbitals, occupations), 'band', scatter_dimen...]
    pallas_call x0 -> x3, Pallas kernels: none -> 16 us  [the longest x1 10.5 us: lateral(): pl.pallas_call(lateral_kernel, grid=(bands,), in_specs=[pl.BlockSpec(memo...]
    sub x4 -> x0, other arithmetic: 15.8 us -> none  [advance(): real_part * derivative(imag_part, direction)]
    slice x10 -> x0, local copies, waits for them, and re-layouts: 14.6 us -> none  [derivative(): forward = jnp.roll(values, -1, direction) - jnp.roll(values, 1, direction)]
    ppermute x2 -> x11, starting transfers between devices: 6.01 us -> 13.6 us  [route(): return lax.ppermute(value, ('band', 'grid'), pairs)]
    ppermute x2 -> x11, waiting for transfers between devices: 21 us -> 28.2 us  [route(): return lax.ppermute(value, ('band', 'grid'), pairs)]
    convert_element_type x6 -> x0, other arithmetic: 7.14 us -> none  [the longest x2 5.46 us: advance(): lax.dynamic_slice_in_dim(padded, offset, block_size, 0).astype(jnp.float32)]
  transfers between devices with their start and end apart: 4 -> 11, of which waited for: 3 -> 5; matrix products, arithmetic and copies ran while one was open for 50% -> 4% of each run, Pallas kernels for 0% -> 4%
where the time goes in v1:
time: 66.2 us; the launch traced here: 65.7 us
  waiting for transfers between devices  28.2 us (43%)
  Pallas kernels  16 us (24%)
  starting transfers between devices  13.6 us (21%)
  local copies, waits for them, and re-layouts  4.86 us (7%)
  other arithmetic  2.95 us (4%)
    ppermute x11, waiting for transfers between devices, route(): return lax.ppermute(value, ('band', 'grid'), pairs)  28.2 us
    ppermute x11, starting transfers between devices, route(): return lax.ppermute(value, ('band', 'grid'), pairs)  13.6 us
    pallas_call x1, Pallas kernels, lateral(): pl.pallas_call(lateral_kernel, grid=(bands,), in_specs=[pl.BlockSpec(memo...  10.5 us
    pallas_call x2, Pallas kernels, call(): pl.pallas_call(kernel, in_specs=[smem] * len(scalars) + [vmem] * len(arra...  5.54 us
    unnamed x18, local copies, waits for them, and re-layouts  2.52 us
    another operation x2, other arithmetic, per_device(): return jnp.stack([depth, flat[1:3], flat[3:5]])  1.42 us
    dynamic_slice x1, local copies, waits for them, and re-layouts, rows(): return lax.dynamic_slice_in_dim(orbitals, index * quarter, quarter, 3)  1.38 us
  transfers between devices with their start and end apart: 11, of which 5 were waited for; matrix products, arithmetic and copies ran while one was open for 4% of the time, Pallas kernels for 4%

profile of v1, /device:TPU:0, one launch (start us, length us, event | category | flops | bytes accessed | tf_op | source)
XLA Modules:
  0.0 65.7 jit_solution(1739883750039619192)
XLA Ops:
  0.0 0.0 copy-start
  0.0 0.0 copy-start.7
  0.0 10.5 %lateral.1 = f32[2,2,5,32,128]{4,3,2,1,0:T(8,128)} custom-call(f32[16]{0:T(128)} %w1.3, bf16[16,2,2,128,128]{4,3,2,1,0:T(8,128)(2,1)} %block.1, bf16[128,128]{1,0:T(8,128)(2,1)} %constant.49.across, bf16[128,128]{1,0:T(8,128)(2,1)} %constant.47.clone.along), custom_call_target="tpu_custom_call" | custom-call | tf_op jit(solution)/shard_map/lateral/pallas_call | solution.py:51
  10.5 0.9 %dynamic-slice_bitcast_fusion = f32[2,5,32,128]{3,2,1,0:T(8,128)S(1)} fusion(f32[2,2,5,32,128]{4,3,2,1,0:T(8,128)} %lateral.1, s32[]{:T(128)S(6)} %select_n.41), kind=kLoop, calls=%fused_computation.1 | loop fusion | bytes 327684 | tf_op jit(solution)/shard_map/squeeze | solution.py:173
  11.4 0.6 collective-permute-start
  12.0 0.0 copy-done.7
  12.0 0.1 collective-permute-start.2
  12.1 0.9 %collective-permute-done = f32[2,5,32,128]{3,2,1,0:T(8,128)S(1)} collective-permute-done((f32[2,5,32,128]{3,2,1,0:T(8,128)S(1)}, f32[2,5,32,128]{3,2,1,0:T(8,128)S(1)}, u32[]{:S(2)}, u32[]{:S(2)}) %collective-permute-start) | collective-permute-done | bytes 163872 | tf_op jit(solution)/shard_map/ppermute | solution.py:155
  13.0 0.9 %bitcast_add_fusion = f32[2,5,32,128]{3,2,1,0:T(8,128)S(1)} fusion(f32[2,5,32,128]{3,2,1,0:T(8,128)S(1)} %collective-permute-done, f32[2,2,5,32,128]{4,3,2,1,0:T(8,128)} %lateral.1, s32[]{:T(128)S(6)} %select_n.40), kind=kLoop, calls=%fused_computation | loop fusion | flops 40960 | bytes 491524 | tf_op jit(solution)/shard_map/add | solution.py:173
  14.0 2.9 %collective-permute-start.1 = (f32[5,32,128]{2,1,0:T(8,128)S(1)}, f32[5,32,128]{2,1,0:T(8,128)S(1)}, u32[]{:S(2)}, u32[]{:S(2)}) collective-permute-start(f32[5,32,128]{2,1,0:T(8,128)S(1)} %dynamic-slice_bitcast_fusion.1), channel_id=1, source_target_pairs={{0,16},{1,17},{2,18},{3,19},{4,20},{5,21},{6,22},{7,23},{8,24},{9,... | collective-permute-start | bytes 245768 | tf_op jit(solution)/shard_map/ppermute | solution.py:155
  16.9 0.0 copy-done
  16.9 1.4 %constant_dynamic-slice_fusion = (bf16[16,2,2,32,128]{4,3,2,1,0:T(8,128)(2,1)}, bf16[16,2,2,32,128]{4,3,2,1,0:T(8,128)(2,1)}, bf16[16,2,2,32,128]{4,3,2,1,0:T(8,128)(2,1)}, bf16[16,2,2,32,128]{4,3,2,1,0:T(8,128)(2,1)S(1)}) fusion(bf16[16,2,2,128,128]{4,3,2,1,0:T(8,128)(2,1)S(1)} %copy-done, s32[]{:T(128)S(6)} %select_n.49, s32[]{:T(128)S(6)} %select_n.47, ...), kind=kLoop, calls=%fused_computation.9 | loop fusion | bytes 4194320 | tf_op jit(solution)/shard_map/dynamic_slice | solution.py:158
  18.3 0.0 copy-start.3
  18.3 0.0 collective-permute-start.7
  18.3 3.7 %collective-permute-start.6 = (bf16[16,2,2,32,128]{4,3,2,1,0:T(8,128)(2,1)}, bf16[16,2,2,32,128]{4,3,2,1,0:T(8,128)(2,1)S(1)}, u32[]{:S(2)}, u32[]{:S(2)}) collective-permute-start(bf16[16,2,2,32,128]{4,3,2,1,0:T(8,128)(2,1)} %get-tuple-element.17), channel_id=1, source_target_pairs={{0,14},{1,11},{2,8},{3,13},{4,10},{5,15},{6,12},{7,9},{8,6},{9,3},... | collective-permute-start | bytes 1572872 | tf_op jit(solution)/shard_map/ppermute | solution.py:155
  22.0 0.0 collective-permute-start.3
  22.0 0.0 collective-permute-done.2.w2
  22.0 0.0 copy-start.8
  22.0 1.3 %collective-permute-start.4 = (bf16[16,2,2,32,128]{4,3,2,1,0:T(8,128)(2,1)}, bf16[16,2,2,32,128]{4,3,2,1,0:T(8,128)(2,1)S(1)}, u32[]{:S(2)}, u32[]{:S(2)}) collective-permute-start(bf16[16,2,2,32,128]{4,3,2,1,0:T(8,128)(2,1)} %get-tuple-element.18), channel_id=1, source_target_pairs={{0,9},{1,8},{2,11},{3,10},{4,13},{5,12},{6,15},{7,14},{8,1},{9,0},... | collective-permute-start | bytes 1572872 | tf_op jit(solution)/shard_map/ppermute | solution.py:155
  23.4 0.0 collective-permute-done.1
  23.4 0.5 collective-permute-start.5
  23.8 0.6 pad_add_fusion.flags
  24.4 12.6 %collective-permute-done.3.side1 = bf16[16,2,2,32,128]{4,3,2,1,0:T(8,128)(2,1)S(1)} collective-permute-done((bf16[16,2,2,32,128]{4,3,2,1,0:T(8,128)(2,1)}, bf16[16,2,2,32,128]{4,3,2,1,0:T(8,128)(2,1)S(1)}, u32[]{:S(2)}, u32[]{:S(2)}) %collective-permute-start.3) | collective-permute-done | bytes 524320 | tf_op jit(solution)/shard_map/ppermute | solution.py:155
  37.0 0.0 copy-start.1
  37.0 9.3 %collective-permute-done.4.side2 = bf16[16,2,2,32,128]{4,3,2,1,0:T(8,128)(2,1)S(1)} collective-permute-done((bf16[16,2,2,32,128]{4,3,2,1,0:T(8,128)(2,1)}, bf16[16,2,2,32,128]{4,3,2,1,0:T(8,128)(2,1)S(1)}, u32[]{:S(2)}, u32[]{:S(2)}) %collective-permute-start.4) | collective-permute-done | bytes 524320 | tf_op jit(solution)/shard_map/ppermute | solution.py:155
  46.3 0.0 copy-start.2
  46.3 0.0 collective-permute-done.7.own2
  46.3 0.0 copy-done.3
  46.3 0.0 copy-done.8
  46.4 0.0 copy-done.1
  46.4 0.8 %copy-done.2 = bf16[16,2,2,32,128]{4,3,2,1,0:T(8,128)(2,1)} copy-done((bf16[16,2,2,32,128]{4,3,2,1,0:T(8,128)(2,1)}, bf16[16,2,2,32,128]{4,3,2,1,0:T(8,128)(2,1)S(1)}, u32[]{:S(2)}) %copy-start.2) | copy-done | bytes 524312
  47.1 0.0 copy-start.6
  47.1 0.8 %copy-done.6 = bf16[16,2,2,32,128]{4,3,2,1,0:T(8,128)(2,1)} copy-done((bf16[16,2,2,32,128]{4,3,2,1,0:T(8,128)(2,1)}, bf16[16,2,2,32,128]{4,3,2,1,0:T(8,128)(2,1)S(1)}, u32[]{:S(2)}) %copy-start.6) | copy-done | bytes 524312
  47.9 2.7 %inner_kernel.1 = (f32[2,32,128]{2,1,0:T(8,128)}, f32[2,32,128]{2,1,0:T(8,128)}) custom-call(s32[2]{0:T(128)} %pad_add_fusion.flags, f32[16]{0:T(128)} %w1.3, f32[16]{0:T(128)} %copy-done.8, bf16[16,2,2,32,128]{4,3,2,1,0:T(8,128)(2,1)} %copy-done.3, bf16[16,2,2,32,128]{4,3,2,1,0:T(8,128)(2,1)} %copy-done.6, bf16[16,2,2,32,128]{4,3,2,1,0:T(8,128)(2,1)} %copy-done.1, ...), custom_call_target="tpu_custom_call" | custom-call | tf_op jit(solution)/shard_map/inner_kernel/pallas_call | solution.py:120
  50.7 0.0 collective-permute-done.5.far1
  50.7 0.0 copy-start.5
  50.7 0.0 collective-permute-done.6.far2
  50.7 0.0 copy-start.4
  50.7 0.8 %copy-done.5 = bf16[16,2,2,32,128]{4,3,2,1,0:T(8,128)(2,1)} copy-done((bf16[16,2,2,32,128]{4,3,2,1,0:T(8,128)(2,1)}, bf16[16,2,2,32,128]{4,3,2,1,0:T(8,128)(2,1)S(1)}, u32[]{:S(2)}) %copy-start.5) | copy-done | bytes 524312
  51.5 0.2 copy-done.4
  51.6 2.8 %outer_kernel.1 = (f32[2,32,128]{2,1,0:T(8,128)}, f32[2,32,128]{2,1,0:T(8,128)}, f32[2,32,128]{2,1,0:T(8,128)}, f32[2,32,128]{2,1,0:T(8,128)}) custom-call(s32[2]{0:T(128)} %pad_add_fusion.flags, f32[16]{0:T(128)} %w1.3, f32[16]{0:T(128)} %copy-done.8, bf16[16,2,2,32,128]{4,3,2,1,0:T(8,128)(2,1)} %copy-done.1, bf16[16,2,2,32,128]{4,3,2,1,0:T(8,128)(2,1)} %copy-done.2, ...), custom_call_target="tpu_custom_call" | custom-call | tf_op jit(solution)/shard_map/outer_kernel/pallas_call | solution.py:120
  54.4 1.3 %collective-permute-start.10 = (f32[2,32,128]{2,1,0:T(8,128)}, f32[2,32,128]{2,1,0:T(8,128)S(1)}, u32[]{:S(2)}, u32[]{:S(2)}) collective-permute-start(f32[2,32,128]{2,1,0:T(8,128)} %get-tuple-element.16), channel_id=1, source_target_pairs={{1,23},{3,17},{5,19},{7,21},{9,31},{11,25},{13,27},{15,29},{16,2},... | collective-permute-start | bytes 98312 | tf_op jit(solution)/shard_map/ppermute | solution.py:155
  55.7 2.7 %collective-permute-start.8 = (f32[2,32,128]{2,1,0:T(8,128)}, f32[2,32,128]{2,1,0:T(8,128)S(1)}, u32[]{:S(2)}, u32[]{:S(2)}) collective-permute-start(f32[2,32,128]{2,1,0:T(8,128)} %get-tuple-element.14), channel_id=1, source_target_pairs={{0,1},{1,17},{2,3},{3,19},{4,5},{5,21},{6,7},{7,23},{8,9},{9,25},{... | collective-permute-start | bytes 98312 | tf_op jit(solution)/shard_map/ppermute | solution.py:155
  58.4 0.6 collective-permute-start.9
  59.0 4.3 %collective-permute-done.10 = f32[2,32,128]{2,1,0:T(8,128)S(1)} collective-permute-done((f32[2,32,128]{2,1,0:T(8,128)}, f32[2,32,128]{2,1,0:T(8,128)S(1)}, u32[]{:S(2)}, u32[]{:S(2)}) %collective-permute-start.10) | collective-permute-done | bytes 32800 | tf_op jit(solution)/shard_map/ppermute | solution.py:155
  63.3 0.0 collective-permute-done.8
  63.3 1.0 %collective-permute-done.9 = f32[2,32,128]{2,1,0:T(8,128)S(1)} collective-permute-done((f32[2,32,128]{2,1,0:T(8,128)}, f32[2,32,128]{2,1,0:T(8,128)S(1)}, u32[]{:S(2)}, u32[]{:S(2)}) %collective-permute-start.9) | collective-permute-done | bytes 32800 | tf_op jit(solution)/shard_map/ppermute | solution.py:155
  64.3 0.8 %add_bitcast_fusion = f32[1,2,32,128]{3,2,1,0:T(8,128)S(1)} fusion(f32[2,32,128]{2,1,0:T(8,128)S(1)} %collective-permute-done.10, f32[2,32,128]{2,1,0:T(8,128)S(1)} %collective-permute-done.9, f32[2,32,128]{2,1,0:T(8,128)S(1)} %collective-permute-done.8, f32[2,32,128]{2,1,0:T(8,128)} %get-tuple-element.13, f32[32,128]{1,0:T(8,128)S(1)} %slice_bitcast_fusion.2), kind=kLoop, calls=%fused_computation.7 | loop fusion | flops 32768 | bytes 180224 | tf_op jit(solution)/shard_map/stack | solution.py:194
  65.1 0.6 pad_maximum_fusion
  (4 shorter events, 0.0 us)
Async XLA Ops:
  0.0 16.9 %copy-start = (bf16[16,2,2,128,128]{4,3,2,1,0:T(8,128)(2,1)S(1)}, bf16[16,2,2,128,128]{4,3,2,1,0:T(8,128)(2,1)}, u32[]{:S(2)}) copy-start(bf16[16,2,2,128,128]{4,3,2,1,0:T(8,128)(2,1)} %block.1) | copy-start | bytes 6291460
  0.0 12.0 %copy-start.7 = (f32[16]{0:T(128)S(1)}, f32[16]{0:T(128)}, u32[]{:S(2)}) copy-start(f32[16]{0:T(128)} %w1.3) | copy-start | bytes 196
  11.4 1.6 %collective-permute-start = (f32[2,5,32,128]{3,2,1,0:T(8,128)S(1)}, f32[2,5,32,128]{3,2,1,0:T(8,128)S(1)}, u32[]{:S(2)}, u32[]{:S(2)}) collective-permute-start(f32[2,5,32,128]{3,2,1,0:T(8,128)S(1)} %dynamic-slice_bitcast_fusion), channel_id=1, source_target_pairs={{0,8},{1,9},{2,10},{3,11},{4,12},{5,13},{6,14},{7,15},{8,0},{9,1},... | collective-permute-start | bytes 491528 | tf_op jit(solution)/shard_map/ppermute | solution.py:155
  12.0 10.0 %collective-permute-start.2 = (f32[16]{0:T(128)S(1)}, f32[16]{0:T(128)S(1)}, u32[]{:S(2)}, u32[]{:S(2)}) collective-permute-start(f32[16]{0:T(128)S(1)} %copy-done.7), channel_id=1, source_target_pairs={{0,8},{1,9},{2,10},{3,11},{4,12},{5,13},{6,14},{7,15},{8,0},{9,1},... | collective-permute-start | bytes 200 | tf_op jit(solution)/shard_map/ppermute | solution.py:155
  14.0 9.4 %collective-permute-start.1 = (f32[5,32,128]{2,1,0:T(8,128)S(1)}, f32[5,32,128]{2,1,0:T(8,128)S(1)}, u32[]{:S(2)}, u32[]{:S(2)}) collective-permute-start(f32[5,32,128]{2,1,0:T(8,128)S(1)} %dynamic-slice_bitcast_fusion.1), channel_id=1, source_target_pairs={{0,16},{1,17},{2,18},{3,19},{4,20},{5,21},{6,22},{7,23},{8,24},{9,... | collective-permute-start | bytes 245768 | tf_op jit(solution)/shard_map/ppermute | solution.py:155
  18.3 28.0 %copy-start.3 = (bf16[16,2,2,32,128]{4,3,2,1,0:T(8,128)(2,1)}, bf16[16,2,2,32,128]{4,3,2,1,0:T(8,128)(2,1)S(1)}, u32[]{:S(2)}) copy-start(bf16[16,2,2,32,128]{4,3,2,1,0:T(8,128)(2,1)S(1)} %get-tuple-element.20.own1) | copy-start | bytes 1572868
  18.3 28.0 %collective-permute-start.7 = (bf16[16,2,2,32,128]{4,3,2,1,0:T(8,128)(2,1)}, bf16[16,2,2,32,128]{4,3,2,1,0:T(8,128)(2,1)S(1)}, u32[]{:S(2)}, u32[]{:S(2)}) collective-permute-start(bf16[16,2,2,32,128]{4,3,2,1,0:T(8,128)(2,1)} %get-tuple-element.17), channel_id=1, source_target_pairs={{0,8},{1,9},{2,10},{3,11},{4,12},{5,13},{6,14},{7,15},{8,0},{9,1},... | collective-permute-start | bytes 1572872 | tf_op jit(solution)/shard_map/ppermute | solution.py:155
  18.3 32.4 %collective-permute-start.6 = (bf16[16,2,2,32,128]{4,3,2,1,0:T(8,128)(2,1)}, bf16[16,2,2,32,128]{4,3,2,1,0:T(8,128)(2,1)S(1)}, u32[]{:S(2)}, u32[]{:S(2)}) collective-permute-start(bf16[16,2,2,32,128]{4,3,2,1,0:T(8,128)(2,1)} %get-tuple-element.17), channel_id=1, source_target_pairs={{0,14},{1,11},{2,8},{3,13},{4,10},{5,15},{6,12},{7,9},{8,6},{9,3},... | collective-permute-start | bytes 1572872 | tf_op jit(solution)/shard_map/ppermute | solution.py:155
  22.0 15.0 %collective-permute-start.3 = (bf16[16,2,2,32,128]{4,3,2,1,0:T(8,128)(2,1)}, bf16[16,2,2,32,128]{4,3,2,1,0:T(8,128)(2,1)S(1)}, u32[]{:S(2)}, u32[]{:S(2)}) collective-permute-start(bf16[16,2,2,32,128]{4,3,2,1,0:T(8,128)(2,1)} %get-tuple-element.19), channel_id=1, source_target_pairs={{0,1},{1,0},{2,3},{3,2},{4,5},{5,4},{6,7},{7,6},{8,9},{9,8},{10,11... | collective-permute-start | bytes 1572872 | tf_op jit(solution)/shard_map/ppermute | solution.py:155
  22.0 24.3 %copy-start.8 = (f32[16]{0:T(128)}, f32[16]{0:T(128)S(1)}, u32[]{:S(2)}) copy-start(f32[16]{0:T(128)S(1)} %collective-permute-done.2.w2) | copy-start | bytes 196
  22.0 24.3 %collective-permute-start.4 = (bf16[16,2,2,32,128]{4,3,2,1,0:T(8,128)(2,1)}, bf16[16,2,2,32,128]{4,3,2,1,0:T(8,128)(2,1)S(1)}, u32[]{:S(2)}, u32[]{:S(2)}) collective-permute-start(bf16[16,2,2,32,128]{4,3,2,1,0:T(8,128)(2,1)} %get-tuple-element.18), channel_id=1, source_target_pairs={{0,9},{1,8},{2,11},{3,10},{4,13},{5,12},{6,15},{7,14},{8,1},{9,0},... | collective-permute-start | bytes 1572872 | tf_op jit(solution)/shard_map/ppermute | solution.py:155
  23.4 27.3 %collective-permute-start.5 = (bf16[16,2,2,32,128]{4,3,2,1,0:T(8,128)(2,1)S(1)}, bf16[16,2,2,32,128]{4,3,2,1,0:T(8,128)(2,1)S(1)}, u32[]{:S(2)}, u32[]{:S(2)}) collective-permute-start(bf16[16,2,2,32,128]{4,3,2,1,0:T(8,128)(2,1)S(1)} %get-tuple-element.20.own1), channel_id=1, source_target_pairs={{0,6},{1,3},{2,0},{3,5},{4,2},{5,7},{6,4},{7,1},{8,14},{9,11},{10,... | collective-permute-start | bytes 1572872 | tf_op jit(solution)/shard_map/ppermute | solution.py:155
  37.0 9.3 %copy-start.1 = (bf16[16,2,2,32,128]{4,3,2,1,0:T(8,128)(2,1)}, bf16[16,2,2,32,128]{4,3,2,1,0:T(8,128)(2,1)S(1)}, u32[]{:S(2)}) copy-start(bf16[16,2,2,32,128]{4,3,2,1,0:T(8,128)(2,1)S(1)} %collective-permute-done.3.side1) | copy-start | bytes 1572868
  46.3 0.8 %copy-start.2 = (bf16[16,2,2,32,128]{4,3,2,1,0:T(8,128)(2,1)}, bf16[16,2,2,32,128]{4,3,2,1,0:T(8,128)(2,1)S(1)}, u32[]{:S(2)}) copy-start(bf16[16,2,2,32,128]{4,3,2,1,0:T(8,128)(2,1)S(1)} %collective-permute-done.4.side2) | copy-start | bytes 1572868
  47.1 0.8 %copy-start.6 = (bf16[16,2,2,32,128]{4,3,2,1,0:T(8,128)(2,1)}, bf16[16,2,2,32,128]{4,3,2,1,0:T(8,128)(2,1)S(1)}, u32[]{:S(2)}) copy-start(bf16[16,2,2,32,128]{4,3,2,1,0:T(8,128)(2,1)S(1)} %collective-permute-done.7.own2) | copy-start | bytes 1572868
  50.7 0.8 %copy-start.5 = (bf16[16,2,2,32,128]{4,3,2,1,0:T(8,128)(2,1)}, bf16[16,2,2,32,128]{4,3,2,1,0:T(8,128)(2,1)S(1)}, u32[]{:S(2)}) copy-start(bf16[16,2,2,32,128]{4,3,2,1,0:T(8,128)(2,1)S(1)} %collective-permute-done.5.far1) | copy-start | bytes 1572868
  50.7 1.0 %copy-start.4 = (bf16[16,2,2,32,128]{4,3,2,1,0:T(8,128)(2,1)}, bf16[16,2,2,32,128]{4,3,2,1,0:T(8,128)(2,1)S(1)}, u32[]{:S(2)}) copy-start(bf16[16,2,2,32,128]{4,3,2,1,0:T(8,128)(2,1)S(1)} %collective-permute-done.6.far2) | copy-start | bytes 1572868
  54.4 8.9 %collective-permute-start.10 = (f32[2,32,128]{2,1,0:T(8,128)}, f32[2,32,128]{2,1,0:T(8,128)S(1)}, u32[]{:S(2)}, u32[]{:S(2)}) collective-permute-start(f32[2,32,128]{2,1,0:T(8,128)} %get-tuple-element.16), channel_id=1, source_target_pairs={{1,23},{3,17},{5,19},{7,21},{9,31},{11,25},{13,27},{15,29},{16,2},... | collective-permute-start | bytes 98312 | tf_op jit(solution)/shard_map/ppermute | solution.py:155
  55.7 7.6 %collective-permute-start.8 = (f32[2,32,128]{2,1,0:T(8,128)}, f32[2,32,128]{2,1,0:T(8,128)S(1)}, u32[]{:S(2)}, u32[]{:S(2)}) collective-permute-start(f32[2,32,128]{2,1,0:T(8,128)} %get-tuple-element.14), channel_id=1, source_target_pairs={{0,1},{1,17},{2,3},{3,19},{4,5},{5,21},{6,7},{7,23},{8,9},{9,25},{... | collective-permute-start | bytes 98312 | tf_op jit(solution)/shard_map/ppermute | solution.py:155
  58.4 5.9 %collective-permute-start.9 = (f32[2,32,128]{2,1,0:T(8,128)}, f32[2,32,128]{2,1,0:T(8,128)S(1)}, u32[]{:S(2)}, u32[]{:S(2)}) collective-permute-start(f32[2,32,128]{2,1,0:T(8,128)} %get-tuple-element.15), channel_id=1, source_target_pairs={{0,2},{1,16},{2,4},{3,18},{4,6},{5,20},{6,0},{7,22},{8,10},{9,24},... | collective-permute-start | bytes 98312 | tf_op jit(solution)/shard_map/ppermute | solution.py:155

commit v2 on v1

--- a/solution.py
+++ b/solution.py
@@ -60,6 +60,7 @@
         out_specs=pl.BlockSpec((2, 2, 5, nx // 4, ny), lambda n: (0, 0, 0, 0, 0)),
         out_shape=jax.ShapeDtypeStruct((2, 2, 5, nx // 4, ny), jnp.float32),
         scratch_shapes=[pltpu.VMEM((5, nx, ny), jnp.float32)],
+        compiler_params=pltpu.CompilerParams(vmem_limit_bytes=8 << 20),
         name="lateral",
     )(weights, orbitals, stencil(nx).T, stencil(ny))
 
@@ -122,7 +123,7 @@
         in_specs=[smem] * len(scalars) + [vmem] * len(arrays),
         out_specs=[vmem] * outs,
         out_shape=[out] * outs,
-        name=kernel.__name__,
+        compiler_params=pltpu.CompilerParams(vmem_limit_bytes=8 << 20),
     )(*scalars, *arrays)
 
 
@@ -162,12 +163,12 @@
     side = rows(2 * (1 - odd) + core)
     side_across = rows(2 * (1 - odd) + 1 - core)
 
+    side1 = route(side, lambda b, g: (b, g ^ 1))
+    far1 = route(own, lambda b, g: (b, beyond(g)))
+    side2 = route(side_across, lambda b, g: (b ^ 1, g ^ 1))
+    far2 = route(own_across, lambda b, g: (b ^ 1, beyond(g)))
+    own2 = route(own_across, lambda b, g: (b ^ 1, g))
     w2 = route(occupations, lambda b, g: (b ^ 1, g))
-    far1 = route(own, lambda b, g: (b, beyond(g)))
-    side1 = route(side, lambda b, g: (b, g ^ 1))
-    far2 = route(own_across, lambda b, g: (b ^ 1, beyond(g)))
-    side2 = route(side_across, lambda b, g: (b ^ 1, g ^ 1))
-    own2 = route(own_across, lambda b, g: (b ^ 1, g))
 
     flat = lateral(orbitals, occupations)
     flat = flat[core] + route(flat[1 - core], lambda b, g: (b ^ 1, g))
@@ -186,9 +187,7 @@
         return b // 2 == g % 2
 
     got = route(distant, lambda b, g: None if is_corner(b, g) else (b ^ 2, home(g)))
-    got_middle = route(
-        middle, lambda b, g: (b, home(g)) if is_corner(b, g) else (b ^ 2, g ^ 1)
-    )
+    got_middle = route(middle, lambda b, g: (b, home(g)) if is_corner(b, g) else (b ^ 2, g ^ 1))
     got_near = route(near, lambda b, g: (b, g ^ 1) if is_corner(b, g) else (b ^ 2, g))
     depth = flat[0][None] + kept + got_near + got_middle + got
     return jnp.stack([depth, flat[1:3], flat[3:5]])

time: 66.2 us -> 55.4 us (0.84)
  Pallas kernels: 16 us -> 6.8 us
  other arithmetic: 2.95 us -> 0.77 us
    pallas_call x1, Pallas kernels: 10.5 us -> 4.48 us  [lateral(): pl.pallas_call(lateral_kernel, grid=(bands,), in_specs=[pl.BlockSpec(memo...]
    pallas_call x2, Pallas kernels: 5.54 us -> 2.31 us  [call(): pl.pallas_call(kernel, in_specs=[smem] * len(scalars) + [vmem] * len(arra...]
    unnamed x18 -> x12, local copies, waits for them, and re-layouts: 2.52 us -> 3.78 us
    add x1, other arithmetic: 0.94 us -> 0.02 us  [per_device(): flat = flat[core] + route(flat[1 - core], lambda b, g: (b ^ 1, g))]
    squeeze x1, local copies, waits for them, and re-layouts: 0.93 us -> 0.02 us  [per_device(): flat = flat[core] + route(flat[1 - core], lambda b, g: (b ^ 1, g))]
    another operation x2, other arithmetic: 1.42 us -> 0.66 us  [per_device(): return jnp.stack([depth, flat[1:3], flat[3:5]])]
  transfers between devices with their start and end apart: 11 -> 11, of which waited for: 5 -> 5; matrix products, arithmetic and copies ran while one was open for 4% -> 3% of each run, Pallas kernels for 4% -> 2%
where the time goes in v2:
time: 55.4 us; the launch traced here: 55.1 us
  waiting for transfers between devices  28.5 us (51%)
  starting transfers between devices  13.6 us (25%)
  Pallas kernels  6.8 us (12%)
  local copies, waits for them, and re-layouts  5.31 us (10%)
  other arithmetic  0.77 us (1%)
    ppermute x11, waiting for transfers between devices, route(): return lax.ppermute(value, ('band', 'grid'), pairs)  28.5 us
    ppermute x11, starting transfers between devices, route(): return lax.ppermute(value, ('band', 'grid'), pairs)  13.6 us
    pallas_call x1, Pallas kernels, lateral(): pl.pallas_call(lateral_kernel, grid=(bands,), in_specs=[pl.BlockSpec(memo...  4.48 us
    unnamed x12, local copies, waits for them, and re-layouts  3.78 us
    pallas_call x2, Pallas kernels, call(): pl.pallas_call(kernel, in_specs=[smem] * len(scalars) + [vmem] * len(arra...  2.31 us
    dynamic_slice x1, local copies, waits for them, and re-layouts, rows(): return lax.dynamic_slice_in_dim(orbitals, index * quarter, quarter, 3)  1.49 us
  transfers between devices with their start and end apart: 11, of which 5 were waited for; matrix products, arithmetic and copies ran while one was open for 3% of the time, Pallas kernels for 2%

profile of v2, /device:TPU:0, one launch (start us, length us, event | category | flops | bytes accessed | tf_op | source)
XLA Modules:
  0.0 55.1 jit_solution(5380297031898468496)
XLA Ops:
  0.0 0.0 copy-start.5
  0.0 0.0 copy-start
  0.0 1.6 %copy-done = bf16[16,2,2,128,128]{4,3,2,1,0:T(8,128)(2,1)S(1)} copy-done((bf16[16,2,2,128,128]{4,3,2,1,0:T(8,128)(2,1)S(1)}, bf16[16,2,2,128,128]{4,3,2,1,0:T(8,128)(2,1)}, u32[]{:S(2)}) %copy-start) | copy-done | bytes 2097176
  1.6 0.0 copy-start.2
  1.6 0.8 %copy-done.2 = bf16[128,128]{1,0:T(8,128)(2,1)S(1)} copy-done((bf16[128,128]{1,0:T(8,128)(2,1)S(1)}, bf16[128,128]{1,0:T(8,128)(2,1)}, u32[]{:S(2)}) %copy-start.2) | copy-done | bytes 32792
  2.4 0.0 copy-start.3
  2.4 0.8 %copy-done.3 = bf16[128,128]{1,0:T(8,128)(2,1)S(1)} copy-done((bf16[128,128]{1,0:T(8,128)(2,1)S(1)}, bf16[128,128]{1,0:T(8,128)(2,1)}, u32[]{:S(2)}) %copy-start.3) | copy-done | bytes 32792
  3.1 0.0 copy-start.4
  3.1 0.7 %copy-done.4 = f32[16]{0:T(128)S(1)} copy-done((f32[16]{0:T(128)S(1)}, f32[16]{0:T(128)}, u32[]{:S(2)}) %copy-start.4) | copy-done | bytes 88
  3.8 0.0 copy-start.1
  3.8 4.5 %lateral.1 = f32[2,2,5,32,128]{4,3,2,1,0:T(8,128)S(1)} custom-call(f32[16]{0:T(128)S(1)} %copy-done.4, bf16[16,2,2,128,128]{4,3,2,1,0:T(8,128)(2,1)S(1)} %copy-done, bf16[128,128]{1,0:T(8,128)(2,1)S(1)} %copy-done.3, bf16[128,128]{1,0:T(8,128)(2,1)S(1)} %copy-done.2), custom_call_target="tpu_custom_call" | custom-call | tf_op jit(solution)/shard_map/lateral/pallas_call | solution.py:51
  8.3 0.6 %collective-permute-start = (f32[2,5,32,128]{3,2,1,0:T(8,128)S(1)}, f32[2,5,32,128]{3,2,1,0:T(8,128)S(1)}, u32[]{:S(2)}, u32[]{:S(2)}) collective-permute-start(f32[2,5,32,128]{3,2,1,0:T(8,128)S(1)} %dynamic-slice_bitcast_fusion), channel_id=1, source_target_pairs={{0,8},{1,9},{2,10},{3,11},{4,12},{5,13},{6,14},{7,15},{8,0},{9,1},... | collective-permute-start | bytes 491528 | tf_op jit(solution)/shard_map/ppermute | solution.py:156
  8.9 0.0 copy-done.5
  8.9 0.1 collective-permute-start.2
  8.9 0.9 %collective-permute-done = f32[2,5,32,128]{3,2,1,0:T(8,128)S(1)} collective-permute-done((f32[2,5,32,128]{3,2,1,0:T(8,128)S(1)}, f32[2,5,32,128]{3,2,1,0:T(8,128)S(1)}, u32[]{:S(2)}, u32[]{:S(2)}) %collective-permute-start) | collective-permute-done | bytes 163872 | tf_op jit(solution)/shard_map/ppermute | solution.py:156
  9.9 2.9 %collective-permute-start.1 = (f32[5,32,128]{2,1,0:T(8,128)S(1)}, f32[5,32,128]{2,1,0:T(8,128)S(1)}, u32[]{:S(2)}, u32[]{:S(2)}) collective-permute-start(f32[5,32,128]{2,1,0:T(8,128)S(1)} %dynamic-slice_bitcast_fusion.1), channel_id=1, source_target_pairs={{0,16},{1,17},{2,18},{3,19},{4,20},{5,21},{6,22},{7,23},{8,24},{9,... | collective-permute-start | bytes 245768 | tf_op jit(solution)/shard_map/ppermute | solution.py:156
  12.9 0.0 copy-done.1
  12.9 1.5 %constant_dynamic-slice_fusion = (bf16[16,2,2,32,128]{4,3,2,1,0:T(8,128)(2,1)S(1)}, bf16[16,2,2,32,128]{4,3,2,1,0:T(8,128)(2,1)}, bf16[16,2,2,32,128]{4,3,2,1,0:T(8,128)(2,1)}, bf16[16,2,2,32,128]{4,3,2,1,0:T(8,128)(2,1)S(1)}) fusion(bf16[16,2,2,128,128]{4,3,2,1,0:T(8,128)(2,1)S(1)} %copy-done.1, s32[]{:T(128)S(6)} %select_n.49, s32[]{:T(128)S(6)} %select_n.47, ...), kind=kLoop, calls=%fused_computation.9 | loop fusion | bytes 4194320 | tf_op jit(solution)/shard_map/dynamic_slice | solution.py:159
  14.4 0.0 collective-permute-start.7
  14.4 3.7 %collective-permute-start.6 = (bf16[16,2,2,32,128]{4,3,2,1,0:T(8,128)(2,1)S(1)}, bf16[16,2,2,32,128]{4,3,2,1,0:T(8,128)(2,1)S(1)}, u32[]{:S(2)}, u32[]{:S(2)}) collective-permute-start(bf16[16,2,2,32,128]{4,3,2,1,0:T(8,128)(2,1)S(1)} %get-tuple-element.17), channel_id=1, source_target_pairs={{0,14},{1,11},{2,8},{3,13},{4,10},{5,15},{6,12},{7,9},{8,6},{9,3},... | collective-permute-start | bytes 1572872 | tf_op jit(solution)/shard_map/ppermute | solution.py:156
  18.1 0.0 collective-permute-start.3
  18.1 0.0 collective-permute-done.2.w2
  18.1 1.4 %collective-permute-start.4 = (bf16[16,2,2,32,128]{4,3,2,1,0:T(8,128)(2,1)}, bf16[16,2,2,32,128]{4,3,2,1,0:T(8,128)(2,1)S(1)}, u32[]{:S(2)}, u32[]{:S(2)}) collective-permute-start(bf16[16,2,2,32,128]{4,3,2,1,0:T(8,128)(2,1)} %get-tuple-element.18), channel_id=1, source_target_pairs={{0,9},{1,8},{2,11},{3,10},{4,13},{5,12},{6,15},{7,14},{8,1},{9,0},... | collective-permute-start | bytes 1572872 | tf_op jit(solution)/shard_map/ppermute | solution.py:156
  19.4 0.0 collective-permute-done.1
  19.4 0.4 collective-permute-start.5
  19.9 0.1 pad_add_fusion.flags
  20.0 13.1 %collective-permute-done.3.side1 = bf16[16,2,2,32,128]{4,3,2,1,0:T(8,128)(2,1)S(1)} collective-permute-done((bf16[16,2,2,32,128]{4,3,2,1,0:T(8,128)(2,1)}, bf16[16,2,2,32,128]{4,3,2,1,0:T(8,128)(2,1)S(1)}, u32[]{:S(2)}, u32[]{:S(2)}) %collective-permute-start.3) | collective-permute-done | bytes 524320 | tf_op jit(solution)/shard_map/ppermute | solution.py:156
  33.1 9.3 %collective-permute-done.4.side2 = bf16[16,2,2,32,128]{4,3,2,1,0:T(8,128)(2,1)S(1)} collective-permute-done((bf16[16,2,2,32,128]{4,3,2,1,0:T(8,128)(2,1)}, bf16[16,2,2,32,128]{4,3,2,1,0:T(8,128)(2,1)S(1)}, u32[]{:S(2)}, u32[]{:S(2)}) %collective-permute-start.4) | collective-permute-done | bytes 524320 | tf_op jit(solution)/shard_map/ppermute | solution.py:156
  42.4 0.0 collective-permute-done.7.own2
  42.4 1.2 %shard_map.46 = (f32[2,32,128]{2,1,0:T(8,128)S(1)}, f32[2,32,128]{2,1,0:T(8,128)S(1)}) custom-call(s32[2]{0:T(128)S(1)} %pad_add_fusion.flags, f32[16]{0:T(128)S(1)} %copy-done.5, f32[16]{0:T(128)S(1)} %collective-permute-done.2.w2, bf16[16,2,2,32,128]{4,3,2,1,0:T(8,128)(2,1)S(1)} %get-tuple-element.20.own1, ...), custom_call_target="tpu_custom_call" | custom-call | tf_op jit(solution)/shard_map/pallas_call | solution.py:121
  43.5 0.0 collective-permute-done.5.far1
  43.6 0.0 collective-permute-done.6.far2
  43.6 1.2 %shard_map.47 = (f32[2,32,128]{2,1,0:T(8,128)S(1)}, f32[2,32,128]{2,1,0:T(8,128)S(1)}, f32[2,32,128]{2,1,0:T(8,128)S(1)}, f32[2,32,128]{2,1,0:T(8,128)S(1)}) custom-call(s32[2]{0:T(128)S(1)} %pad_add_fusion.flags, f32[16]{0:T(128)S(1)} %copy-done.5, f32[16]{0:T(128)S(1)} %collective-permute-done.2.w2, ...), custom_call_target="tpu_custom_call" | custom-call | tf_op jit(solution)/shard_map/pallas_call | solution.py:121
  44.7 1.3 %collective-permute-start.10 = (f32[2,32,128]{2,1,0:T(8,128)S(1)}, f32[2,32,128]{2,1,0:T(8,128)S(1)}, u32[]{:S(2)}, u32[]{:S(2)}) collective-permute-start(f32[2,32,128]{2,1,0:T(8,128)S(1)} %get-tuple-element.16), channel_id=1, source_target_pairs={{1,23},{3,17},{5,19},{7,21},{9,31},{11,25},{13,27},{15,29},{16,2},... | collective-permute-start | bytes 98312 | tf_op jit(solution)/shard_map/ppermute | solution.py:156
  46.0 2.7 %collective-permute-start.8 = (f32[2,32,128]{2,1,0:T(8,128)S(1)}, f32[2,32,128]{2,1,0:T(8,128)S(1)}, u32[]{:S(2)}, u32[]{:S(2)}) collective-permute-start(f32[2,32,128]{2,1,0:T(8,128)S(1)} %get-tuple-element.14), channel_id=1, source_target_pairs={{0,1},{1,17},{2,3},{3,19},{4,5},{5,21},{6,7},{7,23},{8,9},{9,25},{... | collective-permute-start | bytes 98312 | tf_op jit(solution)/shard_map/ppermute | solution.py:156
  48.7 0.6 %collective-permute-start.9 = (f32[2,32,128]{2,1,0:T(8,128)S(1)}, f32[2,32,128]{2,1,0:T(8,128)S(1)}, u32[]{:S(2)}, u32[]{:S(2)}) collective-permute-start(f32[2,32,128]{2,1,0:T(8,128)S(1)} %get-tuple-element.15), channel_id=1, source_target_pairs={{0,2},{1,16},{2,4},{3,18},{4,6},{5,20},{6,0},{7,22},{8,10},{9,24},... | collective-permute-start | bytes 98312 | tf_op jit(solution)/shard_map/ppermute | solution.py:156
  49.3 4.1 %collective-permute-done.10 = f32[2,32,128]{2,1,0:T(8,128)S(1)} collective-permute-done((f32[2,32,128]{2,1,0:T(8,128)S(1)}, f32[2,32,128]{2,1,0:T(8,128)S(1)}, u32[]{:S(2)}, u32[]{:S(2)}) %collective-permute-start.10) | collective-permute-done | bytes 32800 | tf_op jit(solution)/shard_map/ppermute | solution.py:156
  53.4 0.0 collective-permute-done.8
  53.4 1.0 %collective-permute-done.9 = f32[2,32,128]{2,1,0:T(8,128)S(1)} collective-permute-done((f32[2,32,128]{2,1,0:T(8,128)S(1)}, f32[2,32,128]{2,1,0:T(8,128)S(1)}, u32[]{:S(2)}, u32[]{:S(2)}) %collective-permute-start.9) | collective-permute-done | bytes 32800 | tf_op jit(solution)/shard_map/ppermute | solution.py:156
  54.4 0.6 %pad_maximum_fusion = f32[3,2,32,128]{3,2,1,0:T(8,128)} fusion(f32[1,2,32,128]{3,2,1,0:T(8,128)S(1)} %get-tuple-element.22, f32[1,2,32,128]{3,2,1,0:T(8,128)S(1)} %get-tuple-element.21, f32[1,2,32,128]{3,2,1,0:T(8,128)S(1)} %add_bitcast_fusion), kind=kLoop, calls=%fused_computation.2 | loop fusion | flops 49152 | bytes 196608 | tf_op jit(solution)/shard_map/stack | solution.py:193
  (7 shorter events, 0.1 us)
Async XLA Ops:
  0.0 8.9 %copy-start.5 = (f32[16]{0:T(128)S(1)}, f32[16]{0:T(128)}, u32[]{:S(2)}) copy-start(f32[16]{0:T(128)} %w1.3) | copy-start | bytes 196
  0.0 1.6 %copy-start = (bf16[16,2,2,128,128]{4,3,2,1,0:T(8,128)(2,1)S(1)}, bf16[16,2,2,128,128]{4,3,2,1,0:T(8,128)(2,1)}, u32[]{:S(2)}) copy-start(bf16[16,2,2,128,128]{4,3,2,1,0:T(8,128)(2,1)} %block.1) | copy-start | bytes 6291460
  1.6 0.8 %copy-start.2 = (bf16[128,128]{1,0:T(8,128)(2,1)S(1)}, bf16[128,128]{1,0:T(8,128)(2,1)}, u32[]{:S(2)}) copy-start(bf16[128,128]{1,0:T(8,128)(2,1)} %constant.47.clone.along) | copy-start | bytes 98308
  2.4 0.8 %copy-start.3 = (bf16[128,128]{1,0:T(8,128)(2,1)S(1)}, bf16[128,128]{1,0:T(8,128)(2,1)}, u32[]{:S(2)}) copy-start(bf16[128,128]{1,0:T(8,128)(2,1)} %constant.49.across) | copy-start | bytes 98308
  3.1 0.7 %copy-start.4 = (f32[16]{0:T(128)S(1)}, f32[16]{0:T(128)}, u32[]{:S(2)}) copy-start(f32[16]{0:T(128)} %w1.3) | copy-start | bytes 196
  3.8 9.1 %copy-start.1 = (bf16[16,2,2,128,128]{4,3,2,1,0:T(8,128)(2,1)S(1)}, bf16[16,2,2,128,128]{4,3,2,1,0:T(8,128)(2,1)}, u32[]{:S(2)}) copy-start(bf16[16,2,2,128,128]{4,3,2,1,0:T(8,128)(2,1)} %block.1) | copy-start | bytes 6291460
  8.3 1.6 %collective-permute-start = (f32[2,5,32,128]{3,2,1,0:T(8,128)S(1)}, f32[2,5,32,128]{3,2,1,0:T(8,128)S(1)}, u32[]{:S(2)}, u32[]{:S(2)}) collective-permute-start(f32[2,5,32,128]{3,2,1,0:T(8,128)S(1)} %dynamic-slice_bitcast_fusion), channel_id=1, source_target_pairs={{0,8},{1,9},{2,10},{3,11},{4,12},{5,13},{6,14},{7,15},{8,0},{9,1},... | collective-permute-start | bytes 491528 | tf_op jit(solution)/shard_map/ppermute | solution.py:156
  8.9 9.2 %collective-permute-start.2 = (f32[16]{0:T(128)S(1)}, f32[16]{0:T(128)S(1)}, u32[]{:S(2)}, u32[]{:S(2)}) collective-permute-start(f32[16]{0:T(128)S(1)} %copy-done.5), channel_id=1, source_target_pairs={{0,8},{1,9},{2,10},{3,11},{4,12},{5,13},{6,14},{7,15},{8,0},{9,1},... | collective-permute-start | bytes 200 | tf_op jit(solution)/shard_map/ppermute | solution.py:156
  9.9 9.5 %collective-permute-start.1 = (f32[5,32,128]{2,1,0:T(8,128)S(1)}, f32[5,32,128]{2,1,0:T(8,128)S(1)}, u32[]{:S(2)}, u32[]{:S(2)}) collective-permute-start(f32[5,32,128]{2,1,0:T(8,128)S(1)} %dynamic-slice_bitcast_fusion.1), channel_id=1, source_target_pairs={{0,16},{1,17},{2,18},{3,19},{4,20},{5,21},{6,22},{7,23},{8,24},{9,... | collective-permute-start | bytes 245768 | tf_op jit(solution)/shard_map/ppermute | solution.py:156
  14.4 28.0 %collective-permute-start.7 = (bf16[16,2,2,32,128]{4,3,2,1,0:T(8,128)(2,1)S(1)}, bf16[16,2,2,32,128]{4,3,2,1,0:T(8,128)(2,1)S(1)}, u32[]{:S(2)}, u32[]{:S(2)}) collective-permute-start(bf16[16,2,2,32,128]{4,3,2,1,0:T(8,128)(2,1)S(1)} %get-tuple-element.17), channel_id=1, source_target_pairs={{0,8},{1,9},{2,10},{3,11},{4,12},{5,13},{6,14},{7,15},{8,0},{9,1},... | collective-permute-start | bytes 1572872 | tf_op jit(solution)/shard_map/ppermute | solution.py:156
  14.4 29.2 %collective-permute-start.6 = (bf16[16,2,2,32,128]{4,3,2,1,0:T(8,128)(2,1)S(1)}, bf16[16,2,2,32,128]{4,3,2,1,0:T(8,128)(2,1)S(1)}, u32[]{:S(2)}, u32[]{:S(2)}) collective-permute-start(bf16[16,2,2,32,128]{4,3,2,1,0:T(8,128)(2,1)S(1)} %get-tuple-element.17), channel_id=1, source_target_pairs={{0,14},{1,11},{2,8},{3,13},{4,10},{5,15},{6,12},{7,9},{8,6},{9,3},... | collective-permute-start | bytes 1572872 | tf_op jit(solution)/shard_map/ppermute | solution.py:156
  18.1 15.0 %collective-permute-start.3 = (bf16[16,2,2,32,128]{4,3,2,1,0:T(8,128)(2,1)}, bf16[16,2,2,32,128]{4,3,2,1,0:T(8,128)(2,1)S(1)}, u32[]{:S(2)}, u32[]{:S(2)}) collective-permute-start(bf16[16,2,2,32,128]{4,3,2,1,0:T(8,128)(2,1)} %get-tuple-element.19), channel_id=1, source_target_pairs={{0,1},{1,0},{2,3},{3,2},{4,5},{5,4},{6,7},{7,6},{8,9},{9,8},{10,11... | collective-permute-start | bytes 1572872 | tf_op jit(solution)/shard_map/ppermute | solution.py:156
  18.1 24.3 %collective-permute-start.4 = (bf16[16,2,2,32,128]{4,3,2,1,0:T(8,128)(2,1)}, bf16[16,2,2,32,128]{4,3,2,1,0:T(8,128)(2,1)S(1)}, u32[]{:S(2)}, u32[]{:S(2)}) collective-permute-start(bf16[16,2,2,32,128]{4,3,2,1,0:T(8,128)(2,1)} %get-tuple-element.18), channel_id=1, source_target_pairs={{0,9},{1,8},{2,11},{3,10},{4,13},{5,12},{6,15},{7,14},{8,1},{9,0},... | collective-permute-start | bytes 1572872 | tf_op jit(solution)/shard_map/ppermute | solution.py:156
  19.4 24.1 %collective-permute-start.5 = (bf16[16,2,2,32,128]{4,3,2,1,0:T(8,128)(2,1)S(1)}, bf16[16,2,2,32,128]{4,3,2,1,0:T(8,128)(2,1)S(1)}, u32[]{:S(2)}, u32[]{:S(2)}) collective-permute-start(bf16[16,2,2,32,128]{4,3,2,1,0:T(8,128)(2,1)S(1)} %get-tuple-element.20.own1), channel_id=1, source_target_pairs={{0,6},{1,3},{2,0},{3,5},{4,2},{5,7},{6,4},{7,1},{8,14},{9,11},{10,... | collective-permute-start | bytes 1572872 | tf_op jit(solution)/shard_map/ppermute | solution.py:156
  44.7 8.7 %collective-permute-start.10 = (f32[2,32,128]{2,1,0:T(8,128)S(1)}, f32[2,32,128]{2,1,0:T(8,128)S(1)}, u32[]{:S(2)}, u32[]{:S(2)}) collective-permute-start(f32[2,32,128]{2,1,0:T(8,128)S(1)} %get-tuple-element.16), channel_id=1, source_target_pairs={{1,23},{3,17},{5,19},{7,21},{9,31},{11,25},{13,27},{15,29},{16,2},... | collective-permute-start | bytes 98312 | tf_op jit(solution)/shard_map/ppermute | solution.py:156
  46.0 7.4 %collective-permute-start.8 = (f32[2,32,128]{2,1,0:T(8,128)S(1)}, f32[2,32,128]{2,1,0:T(8,128)S(1)}, u32[]{:S(2)}, u32[]{:S(2)}) collective-permute-start(f32[2,32,128]{2,1,0:T(8,128)S(1)} %get-tuple-element.14), channel_id=1, source_target_pairs={{0,1},{1,17},{2,3},{3,19},{4,5},{5,21},{6,7},{7,23},{8,9},{9,25},{... | collective-permute-start | bytes 98312 | tf_op jit(solution)/shard_map/ppermute | solution.py:156
  48.7 5.7 %collective-permute-start.9 = (f32[2,32,128]{2,1,0:T(8,128)S(1)}, f32[2,32,128]{2,1,0:T(8,128)S(1)}, u32[]{:S(2)}, u32[]{:S(2)}) collective-permute-start(f32[2,32,128]{2,1,0:T(8,128)S(1)} %get-tuple-element.15), channel_id=1, source_target_pairs={{0,2},{1,16},{2,4},{3,18},{4,6},{5,20},{6,0},{7,22},{8,10},{9,24},... | collective-permute-start | bytes 98312 | tf_op jit(solution)/shard_map/ppermute | solution.py:156

commit v3 on v0

v3 whole, which is shorter than its diff:
```python
import functools

import jax
import jax.numpy as jnp
import numpy as np
from jax import lax
from jax.experimental import pallas as pl
from jax.experimental.pallas import tpu as pltpu
from jax.sharding import PartitionSpec as P


ODD, CORNER, CORE, HALF = range(4, 8)


def stencil(cells):
    eye = np.eye(cells, dtype=np.float32)
    near = np.roll(eye, 1, 0) - np.roll(eye, -1, 0)
    far = np.roll(eye, 2, 0) - np.roll(eye, -2, 0)
    return jnp.asarray(8.0 * near - far, jnp.bfloat16)


def lateral_kernel(table, weights, *rest):
    quarters, (across, along, kept, sent, spread, field, total) = rest[:4], rest[4:]
    bands, parts, planes, rows, _ = quarters[0].shape
    total[...] = jnp.zeros_like(total)
    dot = functools.partial(jnp.dot, preferred_element_type=jnp.float32)

    def advance(n, carry):
        weight = weights[n]
        for i, quarter in enumerate(quarters):
            at = pl.ds(pl.multiple_of(table[i] * rows, rows), rows)
            for part in range(parts):
                for plane in range(planes):
                    field[part, plane, at] = quarter[n, part, plane]
        fields = []
        for plane in range(planes):
            re16 = field[0, plane]
            im16 = field[1, plane]
            re = weight * re16.astype(jnp.float32)
            im = weight * im16.astype(jnp.float32)
            fields.append((re, im, re16, im16))
            total[1 + plane] += re * dot(across[...], im16) - im * dot(across[...], re16)
            total[3 + plane] += re * dot(im16, along[...]) - im * dot(re16, along[...])
        (re, im, _, _), (_, _, re_up, im_up) = fields
        total[0] += 8.0 * (re * im_up.astype(jnp.float32) - im * re_up.astype(jnp.float32))
        return carry

    lax.fori_loop(0, bands, advance, 0)
    for n in range(bands):
        spread[n : n + 1] = jnp.full((1, spread.shape[1]), weights[n], jnp.float32)
    core = table[CORE]
    for half in range(2):
        for out, row in ((kept, 2 * half + core), (sent, 2 * half + 1 - core)):
            at = pl.ds(pl.multiple_of(row * rows, rows), rows)
            out[half] = total[:, at] * (1.0 / 12.0)


def lateral(quarters, table, weights):
    bands, parts, planes, rows, ny = quarters[0].shape
    nx = 4 * rows
    smem = pl.BlockSpec(memory_space=pltpu.SMEM)
    vmem = pl.BlockSpec(memory_space=pltpu.VMEM)
    return pl.pallas_call(
        lateral_kernel,
        in_specs=[smem] * 2 + [vmem] * 6,
        out_specs=[vmem] * 3,
        out_shape=[jax.ShapeDtypeStruct((2, 5, rows, ny), jnp.float32)] * 2
        + [jax.ShapeDtypeStruct((bands, ny), jnp.float32)],
        scratch_shapes=[
            pltpu.VMEM((parts, planes, nx, ny), quarters[0].dtype),
            pltpu.VMEM((5, nx, ny), jnp.float32),
        ],
        compiler_params=pltpu.CompilerParams(vmem_limit_bytes=8 << 20),
        name="lateral",
    )(table, weights, *quarters, stencil(nx).T, stencil(ny))


def split_kernel(table, orbitals, *rest):
    outs, flags, sem = rest[:4], rest[4], rest[5]
    rows = outs[0].shape[3]
    copies = [
        pltpu.make_async_copy(
            orbitals.at[:, :, :, pl.ds(pl.multiple_of(table[i] * rows, rows), rows)], out, sem.at[i]
        )
        for i, out in enumerate(outs)
    ]
    for copy in copies:
        copy.start()
    for i in range(flags.shape[0]):
        flags[i : i + 1] = jnp.full((1, flags.shape[1]), table[i], jnp.int32)
    for copy in copies:
        copy.wait()


def split(table, orbitals):
    bands, parts, planes, nx, ny = orbitals.shape
    smem = pl.BlockSpec(memory_space=pltpu.SMEM)
    vmem = pl.BlockSpec(memory_space=pltpu.VMEM)
    return pl.pallas_call(
        split_kernel,
        in_specs=[smem, pl.BlockSpec(memory_space=pltpu.HBM)],
        out_specs=[vmem] * 5,
        out_shape=[pltpu.VMEM((bands, parts, planes, nx // 4, ny), orbitals.dtype)] * 4
        + [pltpu.VMEM((8, ny), jnp.int32)],
        scratch_shapes=[pltpu.SemaphoreType.DMA((4,))],
        compiler_params=pltpu.CompilerParams(vmem_limit_bytes=4 << 20),
        name="split",
    )(table, pltpu.with_memory_space_constraint(orbitals, pltpu.HBM))


def halve_kernel(flags, mine, theirs, kept, sent):
    lower = jnp.broadcast_to(flags[HALF : HALF + 1], kept.shape[1:]) == 0
    for i in range(kept.shape[0]):
        low = mine[0, i] + theirs[0, i]
        high = mine[1, i] + theirs[1, i]
        kept[i] = jnp.where(lower, low, high)
        sent[i] = jnp.where(lower, high, low)


def edges(odd, weights, own, side, far, sums):
    def advance(n, sums):
        def field(rows):
            planes = [[rows[n, part, k].astype(jnp.float32) for part in range(2)] for k in range(2)]
            return planes

        def pick(low, high):
            return [jnp.where(odd, a, b) for a, b in zip(low, high)]

        def term(first, second):
            return weight * (first[0] * second[1] - first[1] * second[0])

        weight = weights[pl.ds(n, 1)]
        o, s, f = field(own), field(side), field(far)
        lower = pick(s[0], s[1])
        upper = pick(s[1], s[0])
        new = (
            term(o[0], s[0]),
            term(o[1], s[1]),
            term(pick(o[0], o[1]), upper),
            term(s[0], f[0]),
            term(s[1], f[1]),
            term(lower, pick(f[1], f[0])),
        )
        return tuple(a + b for a, b in zip(sums, new))

    return lax.fori_loop(0, own.shape[0], advance, sums, unroll=UNROLL)


def first_kernel(flags, weights, own, side, far, out):
    zero = jnp.zeros(out.shape[1:], jnp.float32)
    odd = jnp.broadcast_to(flags[ODD : ODD + 1], out.shape[1:]) == 1
    for i, value in enumerate(edges(odd, weights, own, side, far, (zero,) * 6)):
        out[i] = value


def second_kernel(flags, weights, own, side, far, sums, kept, near, middle, distant):
    shape = kept.shape[1:]
    odd = jnp.broadcast_to(flags[ODD : ODD + 1], shape) == 1
    here = jnp.broadcast_to(flags[CORNER : CORNER + 1], shape) == 1
    sums = edges(odd, weights, own, side, far, tuple(sums[i] for i in range(6)))
    up = jnp.where(odd, 1.0, 0.0)
    down = 1.0 - up
    sign = (down - up) * (1.0 / 12.0)
    low, high, mid, far_low, far_high, far_mid = (
        value * (sign if i % 3 < 2 else 8.0 * sign) for i, value in enumerate(sums)
    )
    own_parts = (up * mid - low, down * mid - high)
    side_parts = (
        down * mid - low + up * far_mid - far_low,
        up * mid - high + down * far_mid - far_high,
    )
    far_parts = (down * far_mid - far_low, up * far_mid - far_high)
    for plane in range(2):
        kept[plane] = jnp.where(here, own_parts[plane], 0.0)
        near[plane] = jnp.where(here, side_parts[plane], own_parts[plane])
        middle[plane] = jnp.where(here, far_parts[plane], side_parts[plane])
        distant[plane] = far_parts[plane]


def call(kernel, arrays, out_shapes):
    vmem = pl.BlockSpec(memory_space=pltpu.VMEM)
    return pl.pallas_call(
        kernel,
        in_specs=[vmem] * len(arrays),
        out_specs=[vmem] * len(out_shapes),
        out_shape=[jax.ShapeDtypeStruct(shape, jnp.float32) for shape in out_shapes],
        compiler_params=pltpu.CompilerParams(vmem_limit_bytes=4 << 20),
    )(*arrays)


def finish_kernel(flags, flat, flat_rest, kept, near, middle, distant, out):
    here = jnp.broadcast_to(flags[CORNER : CORNER + 1], flat.shape[1:]) == 1
    for plane in range(2):
        total = flat[0] + flat_rest[0] + kept[plane] + near[plane] + middle[plane]
        out[0, plane] = total + jnp.where(here, distant[plane], 0.0)
        out[1, plane] = flat[1 + plane] + flat_rest[1 + plane]
        out[2, plane] = flat[3 + plane] + flat_rest[3 + plane]


def per_device(orbitals, occupations):
    slabs = lax.axis_size("grid")
    groups = lax.axis_size("band")
    assert groups == 4 and slabs % 2 == 0 and orbitals.shape[2] == 2
    slab = lax.axis_index("grid")
    group = lax.axis_index("band")
    odd = slab % 2
    core = group % 2
    half = group // 2
    corner = (half == odd).astype(odd.dtype)

    def beyond(g):
        return (g + 2) % slabs if g % 2 else (g - 2) % slabs

    def home(g):
        return (g - 2) % slabs if g % 2 else (g + 2) % slabs

    def route(value, target):
        pairs = []
        for b in range(groups):
            for g in range(slabs):
                goal = target(b, g)
                pairs.append((b * slabs + g, goal[0] * slabs + goal[1]))
        return lax.ppermute(value, ("band", "grid"), pairs)

    table = jnp.stack(
        [
            2 * odd + core,
            2 * (1 - odd) + core,
            2 * odd + 1 - core,
            2 * (1 - odd) + 1 - core,
            odd,
            corner,
            core,
            half,
        ]
    ).astype(jnp.int32)
    own, side, own_across, side_across, flags = split(table, orbitals)

    side1 = route(side, lambda b, g: (b, g ^ 1))
    far1 = route(own, lambda b, g: (b, beyond(g)))
    side2 = route(side_across, lambda b, g: (b ^ 1, g ^ 1))
    far2 = route(own_across, lambda b, g: (b ^ 1, beyond(g)))
    own2 = route(own_across, lambda b, g: (b ^ 1, g))

    plane = own.shape[-2:]
    mine, sent, spread = lateral((own, side, own_across, side_across), table, occupations)
    w2 = route(spread, lambda b, g: (b ^ 1, g))
    theirs = route(sent, lambda b, g: (b ^ 1, g))
    flat, sent = call(halve_kernel, (flags, mine, theirs), [(5,) + plane] * 2)
    flat_rest = route(sent, lambda b, g: (b ^ 2, g))

    (sums,) = call(first_kernel, (flags, spread, own, side1, far1), [(6,) + plane])
    kept, near, middle, distant = call(
        second_kernel, (flags, w2, own2, side2, far2, sums), [(2,) + plane] * 4
    )

    def is_corner(b, g):
        return b // 2 == g % 2

    got_near = route(near, lambda b, g: (b, g ^ 1) if is_corner(b, g) else (b ^ 2, g))
    got_middle = route(middle, lambda b, g: (b, home(g)) if is_corner(b, g) else (b ^ 2, g ^ 1))
    got = route(distant, lambda b, g: (b ^ 2, home(g)))
    (out,) = call(finish_kernel, (flags, flat, flat_rest, kept, got_near, got_middle, got), [(3, 2) + plane])
    return out


UNROLL = 4


def solution(mesh):
    placed = (P("band", None, "grid", None, None), P("band"))
    return jax.shard_map(
        per_device,
        mesh=mesh,
        in_specs=placed,
        out_specs=P(None, "grid", "band", None),
        check_vma=False,
    )
```

time: 150 us -> 44.9 us (0.30)
  local copies, waits for them, and re-layouts: 53.9 us -> 0.1 us
  other arithmetic: 33.3 us -> 0 us
  waiting for transfers between devices: 42.4 us -> 24.3 us
  between operations: 13.4 us -> 0.06 us
  Pallas kernels: 0 us -> 8.34 us
  starting transfers between devices: 6.05 us -> 12 us
    concatenate x22 -> x0, local copies, waits for them, and re-layouts: 25.8 us -> none  [the longest x14 14.9 us: derivative(): forward = jnp.roll(values, -1, direction) - jnp.roll(values, 1, direction)]
    reduce_scatter x2 -> x0, waiting for transfers between devices: 21.4 us -> none  [the longest x1 21.4 us: per_device(): lax.psum_scatter(depth_part(orbitals, occupations), 'band', scatter_dimen...]
    sub x4 -> x0, other arithmetic: 15.8 us -> none  [advance(): real_part * derivative(imag_part, direction)]
    slice x10 -> x0, local copies, waits for them, and re-layouts: 14.6 us -> none  [derivative(): forward = jnp.roll(values, -1, direction) - jnp.roll(values, 1, direction)]
    pallas_call x0 -> x6, Pallas kernels: none -> 8.34 us  [the longest x1 4.42 us: lateral(): pl.pallas_call(lateral_kernel, in_specs=[smem] * 2 + [vmem] * 6, out_spec...]
    convert_element_type x6 -> x0, other arithmetic: 7.14 us -> none  [the longest x2 5.46 us: advance(): lax.dynamic_slice_in_dim(padded, offset, block_size, 0).astype(jnp.float32)]
    concatenate x2 -> x0, other arithmetic: 6.91 us -> none  [the longest x1 5.42 us: extended(): jnp.concatenate([lax.ppermute(tail, axis, [(i, (i + 1) % count) for i in...]
    while x12 -> x0, local copies, waits for them, and re-layouts: 6.42 us -> none
  transfers between devices with their start and end apart: 4 -> 11, of which waited for: 3 -> 8; matrix products, arithmetic and copies ran while one was open for 50% -> 0% of each run, Pallas kernels for 0% -> 3%
where the time goes in v3:
time: 44.9 us; the launch traced here: 44.8 us
  waiting for transfers between devices  24.3 us (54%)
  starting transfers between devices  12 us (27%)
  Pallas kernels  8.34 us (19%)
    ppermute x11, waiting for transfers between devices, route(): return lax.ppermute(value, ('band', 'grid'), pairs)  24.3 us
    ppermute x11, starting transfers between devices, route(): return lax.ppermute(value, ('band', 'grid'), pairs)  12 us
    pallas_call x1, Pallas kernels, lateral(): pl.pallas_call(lateral_kernel, in_specs=[smem] * 2 + [vmem] * 6, out_spec...  4.42 us
    pallas_call x1, Pallas kernels, split(): pl.pallas_call(split_kernel, in_specs=[smem, pl.BlockSpec(memory_space=pl...  2.11 us
    pallas_call x4, Pallas kernels, call(): pl.pallas_call(kernel, in_specs=[vmem] * len(arrays), out_specs=[vmem] *...  1.81 us
  transfers between devices with their start and end apart: 11, of which 8 were waited for; matrix products, arithmetic and copies ran while one was open for 0% of the time, Pallas kernels for 3%

profile of v3, /device:TPU:0, one launch (start us, length us, event | category | flops | bytes accessed | tf_op | source)
XLA Modules:
  0.0 44.8 jit_solution(10667294884620282876)
XLA Ops:
  0.0 0.0 copy-start
  0.0 0.0 copy-start.1
  0.0 0.0 copy-start.2
  0.0 0.1 stack.39.table
  0.1 2.1 %split.1 = (bf16[16,2,2,32,128]{4,3,2,1,0:T(8,128)(2,1)S(1)}, bf16[16,2,2,32,128]{4,3,2,1,0:T(8,128)(2,1)S(1)}, bf16[16,2,2,32,128]{4,3,2,1,0:T(8,128)(2,1)S(1)}...) custom-call(s32[8]{0:T(128)S(1)} %stack.39.table, bf16[16,2,2,128,128]{4,3,2,1,0:T(8,128)(2,1)} %orbitals.1), custom_call_target="tpu_custom_call" | custom-call | tf_op jit(solution)/shard_map/split/pallas_call | solution.py:99
  2.2 0.0 copy-done
  2.2 0.0 copy-done.1
  2.2 0.0 copy-done.2
  2.2 4.4 %lateral.1 = (f32[2,5,32,128]{3,2,1,0:T(8,128)S(1)}, f32[2,5,32,128]{3,2,1,0:T(8,128)S(1)}, f32[16,128]{1,0:T(8,128)S(1)}) custom-call(s32[8]{0:T(128)S(1)} %stack.39.table, f32[16]{0:T(128)S(1)} %copy-done.2, bf16[16,2,2,32,128]{4,3,2,1,0:T(8,128)(2,1)S(1)} %get-tuple-element.20.rest_0_.own, bf16[16,2,2,32,128]{4,3,2,1,0:T(8,128)(2,1)S(1)} %get-tuple-element.21.rest_1_, ...), custom_call_target="tpu_custom_call" | custom-call | tf_op jit(solution)/shard_map/lateral/pallas_call | solution.py:63
  6.7 0.6 %collective-permute-start = (f32[2,5,32,128]{3,2,1,0:T(8,128)S(1)}, f32[2,5,32,128]{3,2,1,0:T(8,128)S(1)}, u32[]{:S(2)}, u32[]{:S(2)}) collective-permute-start(f32[2,5,32,128]{3,2,1,0:T(8,128)S(1)} %get-tuple-element.25), channel_id=1, source_target_pairs={{0,8},{1,9},{2,10},{3,11},{4,12},{5,13},{6,14},{7,15},{8,0},{9,1},... | collective-permute-start | bytes 491528 | tf_op jit(solution)/shard_map/ppermute | solution.py:223
  7.3 2.6 %collective-permute-start.6 = (bf16[16,2,2,32,128]{4,3,2,1,0:T(8,128)(2,1)S(1)}, bf16[16,2,2,32,128]{4,3,2,1,0:T(8,128)(2,1)S(1)}, u32[]{:S(2)}, u32[]{:S(2)}) collective-permute-start(bf16[16,2,2,32,128]{4,3,2,1,0:T(8,128)(2,1)S(1)} %get-tuple-element.21.rest_1_), channel_id=1, source_target_pairs={{0,1},{1,0},{2,3},{3,2},{4,5},{5,4},{6,7},{7,6},{8,9},{9,8},{10,11... | collective-permute-start | bytes 1572872 | tf_op jit(solution)/shard_map/ppermute | solution.py:223
  9.8 3.6 %collective-permute-start.7 = (bf16[16,2,2,32,128]{4,3,2,1,0:T(8,128)(2,1)S(1)}, bf16[16,2,2,32,128]{4,3,2,1,0:T(8,128)(2,1)S(1)}, u32[]{:S(2)}, u32[]{:S(2)}) collective-permute-start(bf16[16,2,2,32,128]{4,3,2,1,0:T(8,128)(2,1)S(1)} %get-tuple-element.20.rest_0_.own), channel_id=1, source_target_pairs={{0,6},{1,3},{2,0},{3,5},{4,2},{5,7},{6,4},{7,1},{8,14},{9,11},{10,... | collective-permute-start | bytes 1572872 | tf_op jit(solution)/shard_map/ppermute | solution.py:223
  13.4 0.0 collective-permute-start.4
  13.4 0.2 collective-permute-start.5
  13.7 0.0 collective-permute-done.theirs
  13.7 0.3 collective-permute-start.3
  14.0 8.6 %collective-permute-done.6.side = bf16[16,2,2,32,128]{4,3,2,1,0:T(8,128)(2,1)S(1)} collective-permute-done((bf16[16,2,2,32,128]{4,3,2,1,0:T(8,128)(2,1)S(1)}, bf16[16,2,2,32,128]{4,3,2,1,0:T(8,128)(2,1)S(1)}, u32[]{:S(2)}, u32[]{:S(2)}) %collective-permute-start.6) | collective-permute-done | bytes 524320 | tf_op jit(solution)/shard_map/ppermute | solution.py:223
  22.6 2.0 %collective-permute-start.1 = (f32[5,32,128]{2,1,0:T(8,128)S(1)}, f32[5,32,128]{2,1,0:T(8,128)S(1)}, u32[]{:S(2)}, u32[]{:S(2)}) collective-permute-start(f32[5,32,128]{2,1,0:T(8,128)S(1)} %get-tuple-element.27), channel_id=1, source_target_pairs={{0,16},{1,17},{2,18},{3,19},{4,20},{5,21},{6,22},{7,23},{8,24},{9,... | collective-permute-start | bytes 245768 | tf_op jit(solution)/shard_map/ppermute | solution.py:223
  24.6 1.1 %collective-permute-done.7.far = bf16[16,2,2,32,128]{4,3,2,1,0:T(8,128)(2,1)S(1)} collective-permute-done((bf16[16,2,2,32,128]{4,3,2,1,0:T(8,128)(2,1)S(1)}, bf16[16,2,2,32,128]{4,3,2,1,0:T(8,128)(2,1)S(1)}, u32[]{:S(2)}, u32[]{:S(2)}) %collective-permute-start.7) | collective-permute-done | bytes 524320 | tf_op jit(solution)/shard_map/ppermute | solution.py:223
  25.8 0.0 collective-permute-start.2
  25.8 0.6 %shard_map.47.sums = f32[6,32,128]{2,1,0:T(8,128)S(1)} custom-call(s32[8,128]{1,0:T(8,128)S(1)} %get-tuple-element.19.flags, f32[16,128]{1,0:T(8,128)S(1)} %get-tuple-element.28.weights, bf16[16,2,2,32,128]{4,3,2,1,0:T(8,128)(2,1)S(1)} %get-tuple-element.20.rest_0_.own, bf16[16,2,2,32,128]{4,3,2,1,0:T(8,128)(2,1)S(1)} %collective-permute-done.6.side, ...), custom_call_target="tpu_custom_call" | custom-call | tf_op jit(solution)/shard_map/pallas_call | solution.py:182
  26.3 0.6 %collective-permute-done.2.weights = f32[16,128]{1,0:T(8,128)S(1)} collective-permute-done((f32[16,128]{1,0:T(8,128)S(1)}, f32[16,128]{1,0:T(8,128)S(1)}, u32[]{:S(2)}, u32[]{:S(2)}) %collective-permute-start.2) | collective-permute-done | bytes 8224 | tf_op jit(solution)/shard_map/ppermute | solution.py:223
  26.9 6.4 %collective-permute-done.4.side = bf16[16,2,2,32,128]{4,3,2,1,0:T(8,128)(2,1)S(1)} collective-permute-done((bf16[16,2,2,32,128]{4,3,2,1,0:T(8,128)(2,1)S(1)}, bf16[16,2,2,32,128]{4,3,2,1,0:T(8,128)(2,1)S(1)}, u32[]{:S(2)}, u32[]{:S(2)}) %collective-permute-start.4) | collective-permute-done | bytes 524320 | tf_op jit(solution)/shard_map/ppermute | solution.py:223
  33.3 2.8 %collective-permute-done.5.far = bf16[16,2,2,32,128]{4,3,2,1,0:T(8,128)(2,1)S(1)} collective-permute-done((bf16[16,2,2,32,128]{4,3,2,1,0:T(8,128)(2,1)S(1)}, bf16[16,2,2,32,128]{4,3,2,1,0:T(8,128)(2,1)S(1)}, u32[]{:S(2)}, u32[]{:S(2)}) %collective-permute-start.5) | collective-permute-done | bytes 524320 | tf_op jit(solution)/shard_map/ppermute | solution.py:223
  36.2 0.0 collective-permute-done.3.own
  36.2 0.6 %shard_map.48 = (f32[2,32,128]{2,1,0:T(8,128)S(1)}, f32[2,32,128]{2,1,0:T(8,128)S(1)}, f32[2,32,128]{2,1,0:T(8,128)S(1)}, f32[2,32,128]{2,1,0:T(8,128)S(1)}) custom-call(s32[8,128]{1,0:T(8,128)S(1)} %get-tuple-element.19.flags, f32[16,128]{1,0:T(8,128)S(1)} %collective-permute-done.2.weights, bf16[16,2,2,32,128]{4,3,2,1,0:T(8,128)(2,1)S(1)} %collective-permute-done.3.own, ...), custom_call_target="tpu_custom_call" | custom-call | tf_op jit(solution)/shard_map/pallas_call | solution.py:182
  36.8 0.7 %collective-permute-start.8 = (f32[2,32,128]{2,1,0:T(8,128)S(1)}, f32[2,32,128]{2,1,0:T(8,128)S(1)}, u32[]{:S(2)}, u32[]{:S(2)}) collective-permute-start(f32[2,32,128]{2,1,0:T(8,128)S(1)} %get-tuple-element.30), channel_id=1, source_target_pairs={{0,1},{1,17},{2,3},{3,19},{4,5},{5,21},{6,7},{7,23},{8,9},{9,25},{... | collective-permute-start | bytes 98312 | tf_op jit(solution)/shard_map/ppermute | solution.py:223
  37.5 0.0 collective-permute-start.9
  37.5 1.9 %collective-permute-start.10 = (f32[2,32,128]{2,1,0:T(8,128)S(1)}, f32[2,32,128]{2,1,0:T(8,128)S(1)}, u32[]{:S(2)}, u32[]{:S(2)}) collective-permute-start(f32[2,32,128]{2,1,0:T(8,128)S(1)} %get-tuple-element.32), channel_id=1, source_target_pairs={{0,18},{1,23},{2,20},{3,17},{4,22},{5,19},{6,16},{7,21},{8,26},{9,... | collective-permute-start | bytes 98312 | tf_op jit(solution)/shard_map/ppermute | solution.py:223
  39.4 0.0 collective-permute-done.1.flat_rest
  39.4 1.3 %collective-permute-done.8.near = f32[2,32,128]{2,1,0:T(8,128)S(1)} collective-permute-done((f32[2,32,128]{2,1,0:T(8,128)S(1)}, f32[2,32,128]{2,1,0:T(8,128)S(1)}, u32[]{:S(2)}, u32[]{:S(2)}) %collective-permute-start.8) | collective-permute-done | bytes 32800 | tf_op jit(solution)/shard_map/ppermute | solution.py:223
  40.7 2.5 %collective-permute-done.9.middle = f32[2,32,128]{2,1,0:T(8,128)S(1)} collective-permute-done((f32[2,32,128]{2,1,0:T(8,128)S(1)}, f32[2,32,128]{2,1,0:T(8,128)S(1)}, u32[]{:S(2)}, u32[]{:S(2)}) %collective-permute-start.9) | collective-permute-done | bytes 32800 | tf_op jit(solution)/shard_map/ppermute | solution.py:223
  43.2 0.9 %collective-permute-done.10.distant = f32[2,32,128]{2,1,0:T(8,128)S(1)} collective-permute-done((f32[2,32,128]{2,1,0:T(8,128)S(1)}, f32[2,32,128]{2,1,0:T(8,128)S(1)}, u32[]{:S(2)}, u32[]{:S(2)}) %collective-permute-start.10) | collective-permute-done | bytes 32800 | tf_op jit(solution)/shard_map/ppermute | solution.py:223
  44.1 0.7 %shard_map.49 = f32[3,2,32,128]{3,2,1,0:T(8,128)} custom-call(s32[8,128]{1,0:T(8,128)S(1)} %get-tuple-element.19.flags, f32[5,32,128]{2,1,0:T(8,128)S(1)} %get-tuple-element.26.flat, f32[5,32,128]{2,1,0:T(8,128)S(1)} %collective-permute-done.1.flat_rest, f32[2,32,128]{2,1,0:T(8,128)S(1)} %get-tuple-element.29.kept, ...), custom_call_target="tpu_custom_call" | custom-call | tf_op jit(solution)/shard_map/pallas_call | solution.py:182
  (1 shorter events, 0.0 us)
Async XLA Ops:
  0.0 2.2 %copy-start = (bf16[128,128]{1,0:T(8,128)(2,1)S(1)}, bf16[128,128]{1,0:T(8,128)(2,1)}, u32[]{:S(2)}) copy-start(bf16[128,128]{1,0:T(8,128)(2,1)} %constant.41.rest_4_) | copy-start | bytes 98308
  0.0 2.2 %copy-start.1 = (bf16[128,128]{1,0:T(8,128)(2,1)S(1)}, bf16[128,128]{1,0:T(8,128)(2,1)}, u32[]{:S(2)}) copy-start(bf16[128,128]{1,0:T(8,128)(2,1)} %constant.39.clone.rest_5_) | copy-start | bytes 98308
  0.0 2.2 %copy-start.2 = (f32[16]{0:T(128)S(1)}, f32[16]{0:T(128)}, u32[]{:S(2)}) copy-start(f32[16]{0:T(128)} %weights.1) | copy-start | bytes 196
  6.7 7.0 %collective-permute-start = (f32[2,5,32,128]{3,2,1,0:T(8,128)S(1)}, f32[2,5,32,128]{3,2,1,0:T(8,128)S(1)}, u32[]{:S(2)}, u32[]{:S(2)}) collective-permute-start(f32[2,5,32,128]{3,2,1,0:T(8,128)S(1)} %get-tuple-element.25), channel_id=1, source_target_pairs={{0,8},{1,9},{2,10},{3,11},{4,12},{5,13},{6,14},{7,15},{8,0},{9,1},... | collective-permute-start | bytes 491528 | tf_op jit(solution)/shard_map/ppermute | solution.py:223
  7.3 15.3 %collective-permute-start.6 = (bf16[16,2,2,32,128]{4,3,2,1,0:T(8,128)(2,1)S(1)}, bf16[16,2,2,32,128]{4,3,2,1,0:T(8,128)(2,1)S(1)}, u32[]{:S(2)}, u32[]{:S(2)}) collective-permute-start(bf16[16,2,2,32,128]{4,3,2,1,0:T(8,128)(2,1)S(1)} %get-tuple-element.21.rest_1_), channel_id=1, source_target_pairs={{0,1},{1,0},{2,3},{3,2},{4,5},{5,4},{6,7},{7,6},{8,9},{9,8},{10,11... | collective-permute-start | bytes 1572872 | tf_op jit(solution)/shard_map/ppermute | solution.py:223
  9.8 15.9 %collective-permute-start.7 = (bf16[16,2,2,32,128]{4,3,2,1,0:T(8,128)(2,1)S(1)}, bf16[16,2,2,32,128]{4,3,2,1,0:T(8,128)(2,1)S(1)}, u32[]{:S(2)}, u32[]{:S(2)}) collective-permute-start(bf16[16,2,2,32,128]{4,3,2,1,0:T(8,128)(2,1)S(1)} %get-tuple-element.20.rest_0_.own), channel_id=1, source_target_pairs={{0,6},{1,3},{2,0},{3,5},{4,2},{5,7},{6,4},{7,1},{8,14},{9,11},{10,... | collective-permute-start | bytes 1572872 | tf_op jit(solution)/shard_map/ppermute | solution.py:223
  13.4 19.9 %collective-permute-start.4 = (bf16[16,2,2,32,128]{4,3,2,1,0:T(8,128)(2,1)S(1)}, bf16[16,2,2,32,128]{4,3,2,1,0:T(8,128)(2,1)S(1)}, u32[]{:S(2)}, u32[]{:S(2)}) collective-permute-start(bf16[16,2,2,32,128]{4,3,2,1,0:T(8,128)(2,1)S(1)} %get-tuple-element.23.rest_3_), channel_id=1, source_target_pairs={{0,9},{1,8},{2,11},{3,10},{4,13},{5,12},{6,15},{7,14},{8,1},{9,0},... | collective-permute-start | bytes 1572872 | tf_op jit(solution)/shard_map/ppermute | solution.py:223
  13.4 22.7 %collective-permute-start.5 = (bf16[16,2,2,32,128]{4,3,2,1,0:T(8,128)(2,1)S(1)}, bf16[16,2,2,32,128]{4,3,2,1,0:T(8,128)(2,1)S(1)}, u32[]{:S(2)}, u32[]{:S(2)}) collective-permute-start(bf16[16,2,2,32,128]{4,3,2,1,0:T(8,128)(2,1)S(1)} %get-tuple-element.22.rest_2_), channel_id=1, source_target_pairs={{0,14},{1,11},{2,8},{3,13},{4,10},{5,15},{6,12},{7,9},{8,6},{9,3},... | collective-permute-start | bytes 1572872 | tf_op jit(solution)/shard_map/ppermute | solution.py:223
  13.7 22.5 %collective-permute-start.3 = (bf16[16,2,2,32,128]{4,3,2,1,0:T(8,128)(2,1)S(1)}, bf16[16,2,2,32,128]{4,3,2,1,0:T(8,128)(2,1)S(1)}, u32[]{:S(2)}, u32[]{:S(2)}) collective-permute-start(bf16[16,2,2,32,128]{4,3,2,1,0:T(8,128)(2,1)S(1)} %get-tuple-element.22.rest_2_), channel_id=1, source_target_pairs={{0,8},{1,9},{2,10},{3,11},{4,12},{5,13},{6,14},{7,15},{8,0},{9,1},... | collective-permute-start | bytes 1572872 | tf_op jit(solution)/shard_map/ppermute | solution.py:223
  22.6 16.8 %collective-permute-start.1 = (f32[5,32,128]{2,1,0:T(8,128)S(1)}, f32[5,32,128]{2,1,0:T(8,128)S(1)}, u32[]{:S(2)}, u32[]{:S(2)}) collective-permute-start(f32[5,32,128]{2,1,0:T(8,128)S(1)} %get-tuple-element.27), channel_id=1, source_target_pairs={{0,16},{1,17},{2,18},{3,19},{4,20},{5,21},{6,22},{7,23},{8,24},{9,... | collective-permute-start | bytes 245768 | tf_op jit(solution)/shard_map/ppermute | solution.py:223
  25.8 1.2 %collective-permute-start.2 = (f32[16,128]{1,0:T(8,128)S(1)}, f32[16,128]{1,0:T(8,128)S(1)}, u32[]{:S(2)}, u32[]{:S(2)}) collective-permute-start(f32[16,128]{1,0:T(8,128)S(1)} %get-tuple-element.28.weights), channel_id=1, source_target_pairs={{0,8},{1,9},{2,10},{3,11},{4,12},{5,13},{6,14},{7,15},{8,0},{9,1},... | collective-permute-start | bytes 24584 | tf_op jit(solution)/shard_map/ppermute | solution.py:223
  36.8 4.0 %collective-permute-start.8 = (f32[2,32,128]{2,1,0:T(8,128)S(1)}, f32[2,32,128]{2,1,0:T(8,128)S(1)}, u32[]{:S(2)}, u32[]{:S(2)}) collective-permute-start(f32[2,32,128]{2,1,0:T(8,128)S(1)} %get-tuple-element.30), channel_id=1, source_target_pairs={{0,1},{1,17},{2,3},{3,19},{4,5},{5,21},{6,7},{7,23},{8,9},{9,25},{... | collective-permute-start | bytes 98312 | tf_op jit(solution)/shard_map/ppermute | solution.py:223
  37.5 5.7 %collective-permute-start.9 = (f32[2,32,128]{2,1,0:T(8,128)S(1)}, f32[2,32,128]{2,1,0:T(8,128)S(1)}, u32[]{:S(2)}, u32[]{:S(2)}) collective-permute-start(f32[2,32,128]{2,1,0:T(8,128)S(1)} %get-tuple-element.31), channel_id=1, source_target_pairs={{0,2},{1,16},{2,4},{3,18},{4,6},{5,20},{6,0},{7,22},{8,10},{9,24},... | collective-permute-start | bytes 98312 | tf_op jit(solution)/shard_map/ppermute | solution.py:223
  37.5 6.6 %collective-permute-start.10 = (f32[2,32,128]{2,1,0:T(8,128)S(1)}, f32[2,32,128]{2,1,0:T(8,128)S(1)}, u32[]{:S(2)}, u32[]{:S(2)}) collective-permute-start(f32[2,32,128]{2,1,0:T(8,128)S(1)} %get-tuple-element.32), channel_id=1, source_target_pairs={{0,18},{1,23},{2,20},{3,17},{4,22},{5,19},{6,16},{7,21},{8,26},{9,... | collective-permute-start | bytes 98312 | tf_op jit(solution)/shard_map/ppermute | solution.py:223
